TPU v7x, 32 devices: a whole 2x2x4 slice. The times are simulated.
32 devices in a mesh: dp: 8 (over z, x), seq: 4 (over y, core).
Axes of the slice: x: 2, y: 2, z: 4, core: 2. Of those that a mesh axis runs over, the one named last changes fastest.
Arguments:
- hidden: bfloat16 [8, 4096, 4096], P('dp', 'seq'), may hold values from -6 to 6
- value_weight: bfloat16 [4096, 64], replicated, may hold values from -0.09375 to 0.09375
- value_bias: float32 [64], replicated, may hold values from -1 to 1
- returns: float32 [8, 4096], P('dp', 'seq'), may hold values from -12 to 12, as said below
- task_bins: int32 [8, 4096], P('dp', 'seq'), may hold values from 0 to 63
- loss_mask: int32 [8, 4096], P('dp', 'seq'), may hold values 0 or 1
Outputs:
- targets: float32 [8, 4096], P('dp', 'seq')
- weight_grad: float32 [4096, 64], replicated
- bias_grad: float32 [64], replicated
Inputs may be any that keep to these rules, and one draw needn't show every extreme that they name: The returns of one rollout share a level and a trend along positions.
All inputs are finite; a program needn't handle non-finite values.
Results may differ from a plain program's by a relative error of at most 0.00083.
Values sent between devices are 32-bit elements.
No kernel may reach another device: no remote copies, remote signals or barrier semaphores. Data moves between devices by JAX's collectives and lax.ppermute only.
A program may use at most 64 MiB of HBM per device.

v0:
```python
import jax
import jax.numpy as jnp
from jax import lax
from jax.sharding import PartitionSpec as P


def on_device(hidden, value_weight, value_bias, returns, task_bins, loss_mask):
    rollouts = hidden.shape[0] * lax.axis_size("dp")
    states = hidden.reshape(-1, hidden.shape[2])
    flat_returns = returns.reshape(-1)
    bins_iota = jnp.arange(value_weight.shape[1], dtype=jnp.int32)
    chosen = (task_bins.reshape(-1)[:, None] == bins_iota).astype(jnp.float32)
    valid = loss_mask.reshape(-1).astype(jnp.float32)
    onehot = chosen * valid[:, None]
    scores = jnp.dot(states, value_weight, preferred_element_type=jnp.float32)
    counts = jnp.sum(onehot, axis=0)
    summed = jnp.sum(onehot * flat_returns[:, None], axis=0)
    squares = jnp.sum(onehot * flat_returns[:, None] * flat_returns[:, None], axis=0)
    counts, summed, squares = lax.psum((counts, summed, squares), ("dp", "seq"))
    means = summed / jnp.maximum(counts, 1.0)
    second = squares - summed * means
    floor_counts = jnp.maximum(counts, 1.0)
    spread = jnp.sqrt(second / floor_counts + 0.1)
    deviation = flat_returns[:, None] - means
    targets = jnp.sum(chosen * (deviation / spread), axis=-1)
    predicted = jnp.sum((scores + value_bias) * chosen, axis=-1)
    slope = valid * jnp.clip(predicted - targets, -1.0, 1.0) / rollouts
    coefficient = chosen * slope[:, None]
    weight_grad = lax.dot_general(
        states,
        coefficient.astype(jnp.bfloat16),
        (((0,), (0,)), ((), ())),
        preferred_element_type=jnp.float32,
    )
    bias_grad = jnp.sum(coefficient, axis=0)
    weight_grad, bias_grad = lax.psum((weight_grad, bias_grad), ("dp", "seq"))
    return (targets.reshape(returns.shape), weight_grad, bias_grad)


def solution(mesh):
    placed = (P("dp", "seq", None), P(), P(), P("dp", "seq"), P("dp", "seq"), P("dp", "seq"))
    return jax.shard_map(
        on_device, mesh=mesh, in_specs=placed, out_specs=(P("dp", "seq"), P(), P()), check_vma=False
    )
```

profile of v0, /device:TPU:0, one launch (start us, length us, event | category | flops | bytes accessed | tf_op | source)
XLA Modules:
  0.0 201.0 jit_solution(13949442704553326158)
XLA Ops:
  7.2 0.0 copy-start
  7.2 0.0 copy-start.2
  7.2 0.0 all-reduce.3.cloned.1.call-start
  7.2 0.7 convert_element_type.17
  8.0 0.9 fusion.17
  8.9 42.0 %all-reduce = (f32[64]{0:T(128)S(1)}, f32[64]{0:T(128)S(1)}, f32[64]{0:T(128)S(1)}) all-reduce(f32[64]{0:T(128)S(1)} %get-tuple-element.4, f32[64]{0:T(128)S(1)} %get-tuple-element.3, f32[64]{0:T(128)S(1)} %get-tuple-element.5), channel_id=1, replica_groups=mesh['dp'=8,'seq'=4] {'dp','seq'}, use_global_device_ids=true, to_apply=%region_5.0 | all-reduce | flops 192 | bytes 1536 | tf_op jit(solution)/shard_map/psum | solution.py:19
  50.9 0.0 copy-start.1
  50.9 1.0 select_reduce_fusion.2
  51.9 0.0 copy-done
  51.9 0.0 copy-start.3
  51.9 6.3 %fusion.13 = f32[1024]{0:T(1024)S(1)} fusion(bf16[4096,64]{0,1:T(8,128)(2,1)S(1)} %copy-done, bf16[1,1024,4096]{2,1,0:T(8,128)(2,1)} %param.6, f32[64]{0:T(128)} %param.8, s32[1024]{0:T(1024)} %bitcast.22), kind=kOutput, calls=%fused_computation.7 | convolution fusion | flops 537132032 | bytes 8921344 | tf_op jit(solution)/shard_map/dot_general | solution.py:15
  58.2 0.0 copy-done.2
  58.2 0.0 copy-done.1
  58.3 2.5 %fusion.4 = f32[4096,64]{0,1:T(8,128)} fusion(bf16[1,1024,4096]{2,1,0:T(8,128)(2,1)S(1)} %copy-done.1, f32[1024]{0:T(1024)S(1)} %multiply_multiply_fusion, s32[1024]{0:T(1024)S(1)} %bitcast.23), kind=kOutput, calls=%fused_computation.4 | convolution fusion | flops 537001984 | bytes 9445376 | tf_op jit(solution)/shard_map/dot_general | solution.py:29
  60.8 0.0 copy-done.3
  60.8 0.0 all-reduce.3.cloned.1.call-update
  60.8 0.1 select_reduce_fusion
  61.0 40.3 %psum.39 = f32[64]{0:T(128)} all-reduce(f32[64]{0:T(128)S(1)} %select_reduce_fusion), channel_id=1, replica_groups=mesh['dp'=8,'seq'=4] {'dp','seq'}, use_global_device_ids=true, to_apply=%region_10.11 | all-reduce | flops 64 | bytes 512 | tf_op jit(solution)/shard_map/psum | solution.py:36
  101.3 90.6 %all-reduce.3.cloned.1.call-done = f32[4096,64]{0,1:T(8,128)} async-done(((f32[4096,64]{0,1:T(8,128)}), f32[4096,64]{0,1:T(8,128)}) %all-reduce.3.cloned.1.call-update) | async-done | bytes 1048592 | tf_op jit(solution)/shard_map/psum | solution.py:36
  191.9 2.3 %copy.10 = f32[4096,64]{0,1:T(8,128)} copy(f32[4096,64]{0,1:T(8,128)} %all-reduce.3.cloned.1.call-done) | data formatting | bytes 2097152
  (2 shorter events, 0.0 us)
Async XLA Ops:
  7.2 44.8 %copy-start = (bf16[4096,64]{0,1:T(8,128)(2,1)S(1)}, bf16[4096,64]{0,1:T(8,128)(2,1)}, u32[]{:S(2)}) copy-start(bf16[4096,64]{0,1:T(8,128)(2,1)} %param.7) | copy-start | bytes 1572868
  7.2 51.1 %copy-start.2 = (s32[1,1024]{1,0:T(1,128)S(1)}, s32[1,1024]{1,0:T(1,128)}, u32[]{:S(2)}) copy-start(s32[1,1024]{1,0:T(1,128)} %param.10) | copy-start | bytes 12292
  7.2 184.7 %all-reduce.3.cloned.1.call-start = ((), (), s32[]{:S(2)}) async-start(), calls=%async_computation | async-start | bytes 2097152 | tf_op jit(solution)/shard_map/psum | solution.py:36
  50.9 7.3 %copy-start.1 = (bf16[1,1024,4096]{2,1,0:T(8,128)(2,1)S(1)}, bf16[1,1024,4096]{2,1,0:T(8,128)(2,1)}, u32[]{:S(2)}) copy-start(bf16[1,1024,4096]{2,1,0:T(8,128)(2,1)} %param.6) | copy-start | bytes 25165828
  51.9 8.9 %copy-start.3 = (f32[1024]{0:T(1024)}, f32[1024]{0:T(1024)S(1)}, u32[]{:S(2)}) copy-start(f32[1024]{0:T(1024)S(1)} %select_reduce_fusion.2) | copy-start | bytes 12292
Sparse Core Ops, SparseCore 0:
  60.9 130.8 all-reduce.2
where the time goes:
time: 202 us; the launch traced here: 201 us
  waiting for transfers between devices  90.6 us (45%)
  blocking collectives  82.4 us (41%)
  between operations  14.1 us (7%)
  matrix products  8.82 us (4%)
  other arithmetic  2.77 us (1%)
  local copies, waits for them, and re-layouts  2.3 us (1%)
    psum x1, waiting for transfers between devices, on_device(): weight_grad, bias_grad = lax.psum((weight_grad, bias_grad), ('dp', 'seq'))  90.6 us
    psum x1, blocking collectives, on_device(): counts, summed, squares = lax.psum((counts, summed, squares), ('dp', 'seq'))  42 us
    psum x1, blocking collectives, on_device(): weight_grad, bias_grad = lax.psum((weight_grad, bias_grad), ('dp', 'seq'))  40.3 us
    dot_general x1, matrix products, on_device(): scores = jnp.dot(states, value_weight, preferred_element_type=jnp.float32)  6.27 us
  transfers between devices with their start and end apart: 1, of which 1 were waited for; matrix products, arithmetic and copies ran while one was open for 0% of the time, Pallas kernels for 0%

commit v1 on v0

v1 whole, which is shorter than its diff:
```python
import jax
import jax.numpy as jnp
from jax import lax
from jax.sharding import PartitionSpec as P

LANES = 128
SUBLANES = 8


def exchange_rounds(sizes):
    rounds = []
    for axis, widest in (("seq", 2), ("dp", 4)):
        stride, left = 1, sizes[axis]
        while left > 1:
            wanted = 2 if stride == 1 else widest
            radix = next(r for r in [wanted, 2] + list(range(3, left + 1)) if left % r == 0)
            rounds.append((axis, stride, radix))
            stride, left = stride * radix, left // radix
    return rounds


def shift(value, axis, stride, radix, by):
    pairs = []
    for source in range(lax.axis_size(axis)):
        digit = (source // stride) % radix
        pairs.append((source, source + ((digit + by) % radix - digit) * stride))
    return lax.ppermute(value, axis, pairs)


def sum_small(value, rounds):
    for axis, stride, radix in rounds:
        pieces = [shift(value, axis, stride, radix, by) for by in range(1, radix)]
        for piece in pieces:
            value = value + piece
    return value


def binary(rounds, sizes):
    split = []
    for axis, stride, radix in rounds:
        while radix % 2 == 0 and radix > 2:
            split.append((axis, stride, 2))
            stride, radix = stride * 2, radix // 2
        split.append((axis, stride, radix))
    return split


def digit_of(axis, stride, radix):
    return (lax.axis_index(axis) // stride) % radix


def scatter_sum(tiles, extra, rounds):
    for axis, stride, radix in rounds:
        mine = digit_of(axis, stride, radix)
        count = tiles.shape[0] // radix
        got = []
        for by in range(1, radix):
            part = lax.dynamic_slice_in_dim(tiles, ((mine + by) % radix) * count, count, 0)
            got.append(shift(jnp.concatenate([part, extra], axis=0), axis, stride, radix, by))
        tiles = lax.dynamic_slice_in_dim(tiles, mine * count, count, 0)
        for piece in got:
            tiles = tiles + piece[:count]
            extra = extra + piece[count:]
    return tiles, extra


def gather(tiles, rounds):
    for axis, stride, radix in reversed(rounds):
        mine = digit_of(axis, stride, radix)
        count = tiles.shape[0]
        got = [shift(tiles, axis, stride, radix, by) for by in range(1, radix)]
        whole = jnp.zeros((count * radix,) + tiles.shape[1:], tiles.dtype)
        whole = lax.dynamic_update_slice_in_dim(whole, tiles, mine * count, 0)
        for by in range(1, radix):
            whole = lax.dynamic_update_slice_in_dim(whole, got[by - 1], ((mine - by) % radix) * count, 0)
        tiles = whole
    return tiles


def on_device(hidden, value_weight, value_bias, returns, task_bins, loss_mask):
    sizes = {axis: lax.axis_size(axis) for axis in ("dp", "seq")}
    rounds = exchange_rounds(sizes)
    rollouts = hidden.shape[0] * sizes["dp"]
    width, tasks = value_weight.shape
    states = hidden.reshape(-1, width)
    flat_returns = returns.reshape(-1)
    bins_iota = jnp.arange(tasks, dtype=jnp.int32)
    chosen = (task_bins.reshape(-1)[:, None] == bins_iota).astype(jnp.float32)
    valid = loss_mask.reshape(-1).astype(jnp.float32)
    onehot = chosen * valid[:, None]
    counts = jnp.sum(onehot, axis=0)
    summed = jnp.sum(onehot * flat_returns[:, None], axis=0)
    squares = jnp.sum(onehot * flat_returns[:, None] * flat_returns[:, None], axis=0)
    counts, summed, squares = sum_small(jnp.stack([counts, summed, squares]), binary(rounds, sizes))
    scores = jnp.dot(states, value_weight, preferred_element_type=jnp.float32)
    predicted = jnp.sum((scores + value_bias) * chosen, axis=-1)
    floor_counts = jnp.maximum(counts, 1.0)
    means = summed / floor_counts
    second = squares - summed * means
    spread = jnp.sqrt(second / floor_counts + 0.1)
    deviation = flat_returns[:, None] - means
    targets = jnp.sum(chosen * (deviation / spread), axis=-1)
    slope = valid * jnp.clip(predicted - targets, -1.0, 1.0) / rollouts
    coefficient = chosen * slope[:, None]
    weight_grad = lax.dot_general(
        coefficient.astype(jnp.bfloat16),
        states,
        (((0,), (0,)), ((), ())),
        preferred_element_type=jnp.float32,
    )
    bias_grad = jnp.sum(coefficient, axis=0)
    up, across = tasks // SUBLANES, width // LANES
    tiles = weight_grad.reshape(up, SUBLANES, across, LANES).transpose(0, 2, 1, 3)
    tiles = tiles.reshape(up * across, SUBLANES, LANES)
    extra = jnp.zeros((SUBLANES, LANES), jnp.float32).at[0, :tasks].set(bias_grad)[None]
    tiles, extra = scatter_sum(tiles, extra, rounds)
    tiles = gather(tiles, rounds)
    weight_grad = tiles.reshape(up, across, SUBLANES, LANES).transpose(0, 2, 1, 3)
    weight_grad = weight_grad.reshape(tasks, width).T
    return (targets.reshape(returns.shape), weight_grad, extra[0, 0, :tasks])


def solution(mesh):
    placed = (P("dp", "seq", None), P(), P(), P("dp", "seq"), P("dp", "seq"), P("dp", "seq"))
    return jax.shard_map(
        on_device, mesh=mesh, in_specs=placed, out_specs=(P("dp", "seq"), P(), P()), check_vma=False
    )
```

time: 202 us -> 86.7 us (0.43)
  blocking collectives: 82.4 us -> 0 us
  waiting for transfers between devices: 90.6 us -> 36.3 us
  starting transfers between devices: 0.04 us -> 20.5 us
  between operations: 14.1 us -> 0.97 us
  local copies, waits for them, and re-layouts: 2.3 us -> 14.1 us
  matrix products: 8.82 us -> 12.1 us
    psum x1 -> x0, waiting for transfers between devices: 90.6 us -> none  [on_device(): weight_grad, bias_grad = lax.psum((weight_grad, bias_grad), ('dp', 'seq'))]
    psum x2 -> x0, blocking collectives: 82.4 us -> none  [the longest x1 42 us: on_device(): counts, summed, squares = lax.psum((counts, summed, squares), ('dp', 'seq'))]
    ppermute x0 -> x17, waiting for transfers between devices: none -> 36.3 us  [shift(): return lax.ppermute(value, axis, pairs)]
    ppermute x0 -> x17, starting transfers between devices: none -> 20.5 us  [shift(): return lax.ppermute(value, axis, pairs)]
    dot_general x0 -> x1, local copies, waits for them, and re-layouts: none -> 12 us  [on_device(): lax.dot_general(coefficient.astype(jnp.bfloat16), states, (((0,), (0,)),...]
    dot_general x1, matrix products: 2.54 us -> 6.04 us  [on_device(): lax.dot_general(coefficient.astype(jnp.bfloat16), states, (((0,), (0,)),...]
  transfers between devices with their start and end apart: 1 -> 17, of which waited for: 1 -> 15; matrix products, arithmetic and copies ran while one was open for 0% -> 22% of each run, Pallas kernels for 0% -> 0%
where the time goes in v1:
time: 86.7 us; the launch traced here: 86.2 us
  waiting for transfers between devices  36.3 us (42%)
  starting transfers between devices  20.5 us (24%)
  local copies, waits for them, and re-layouts  14.1 us (16%)
  matrix products  12.1 us (14%)
  other arithmetic  2.2 us (3%)
  between operations  0.97 us (1%)
    ppermute x17, waiting for transfers between devices, shift(): return lax.ppermute(value, axis, pairs)  36.3 us
    ppermute x17, starting transfers between devices, shift(): return lax.ppermute(value, axis, pairs)  20.5 us
    dot_general x1, local copies, waits for them, and re-layouts, on_device(): lax.dot_general(coefficient.astype(jnp.bfloat16), states, (((0,), (0,)),...  12 us
    dot_general x1, matrix products, on_device(): scores = jnp.dot(states, value_weight, preferred_element_type=jnp.float32)  6.07 us
    dot_general x1, matrix products, on_device(): lax.dot_general(coefficient.astype(jnp.bfloat16), states, (((0,), (0,)),...  6.04 us
  transfers between devices with their start and end apart: 17, of which 15 were waited for; matrix products, arithmetic and copies ran while one was open for 22% of the time, Pallas kernels for 0%

profile of v1, /device:TPU:0, one launch (start us, length us, event | category | flops | bytes accessed | tf_op | source)
XLA Modules:
  0.0 86.2 jit_solution(6703710601713509495)
XLA Ops:
  3.7 2.9 %collective-permute-start.1 = (f32[3,64]{1,0:T(4,128)S(1)}, f32[3,64]{1,0:T(4,128)S(1)}, u32[]{:S(2)}, u32[]{:S(2)}) collective-permute-start(f32[3,64]{1,0:T(4,128)S(1)} %fusion.22), channel_id=1, source_target_pairs={{0,2},{1,3},{2,0},{3,1},{4,6},{5,7},{6,4},{7,5},{8,10},{9,11},{10,... | collective-permute-start | bytes 2312 | tf_op jit(solution)/shard_map/ppermute | solution.py:27
  6.6 6.1 %fusion.8 = f32[1024]{0:T(1024)S(1)} fusion(bf16[4096,64]{0,1:T(8,128)(2,1)S(1)} %copy-done, bf16[1,1024,4096]{2,1,0:T(8,128)(2,1)} %param.8, f32[64]{0:T(128)} %param.10, s32[1024]{0:T(1024)} %bitcast.51), kind=kOutput, calls=%fused_computation.4 | convolution fusion | flops 537132032 | bytes 8921344 | tf_op jit(solution)/shard_map/dot_general | solution.py:95
  12.7 1.6 %collective-permute-start.2 = (f32[3,64]{1,0:T(4,128)S(1)}, f32[3,64]{1,0:T(4,128)S(1)}, u32[]{:S(2)}, u32[]{:S(2)}) collective-permute-start(f32[3,64]{1,0:T(4,128)S(1)} %fusion.25), channel_id=1, source_target_pairs={{0,4},{4,0},{8,12},{12,8},{16,20},{20,16},{24,28},{28,24},{1,5},{5... | collective-permute-start | bytes 2312 | tf_op jit(solution)/shard_map/ppermute | solution.py:27
  14.3 2.1 %collective-permute-done.2 = f32[3,64]{1,0:T(4,128)S(1)} collective-permute-done((f32[3,64]{1,0:T(4,128)S(1)}, f32[3,64]{1,0:T(4,128)S(1)}, u32[]{:S(2)}, u32[]{:S(2)}) %collective-permute-start.2) | collective-permute-done | bytes 800 | tf_op jit(solution)/shard_map/ppermute | solution.py:27
  16.4 1.6 %collective-permute-start.3 = (f32[3,64]{1,0:T(4,128)S(1)}, f32[3,64]{1,0:T(4,128)S(1)}, u32[]{:S(2)}, u32[]{:S(2)}) collective-permute-start(f32[3,64]{1,0:T(4,128)S(1)} %add.210), channel_id=1, source_target_pairs={{0,8},{4,12},{8,0},{12,4},{16,24},{20,28},{24,16},{28,20},{1,9},{5... | collective-permute-start | bytes 2312 | tf_op jit(solution)/shard_map/ppermute | solution.py:27
  18.0 2.0 %collective-permute-done.3 = f32[3,64]{1,0:T(4,128)S(1)} collective-permute-done((f32[3,64]{1,0:T(4,128)S(1)}, f32[3,64]{1,0:T(4,128)S(1)}, u32[]{:S(2)}, u32[]{:S(2)}) %collective-permute-start.3) | collective-permute-done | bytes 800 | tf_op jit(solution)/shard_map/ppermute | solution.py:27
  20.0 2.6 %collective-permute-start.4 = (f32[3,64]{1,0:T(4,128)S(1)}, f32[3,64]{1,0:T(4,128)S(1)}, u32[]{:S(2)}, u32[]{:S(2)}) collective-permute-start(f32[3,64]{1,0:T(4,128)S(1)} %add.211), channel_id=1, source_target_pairs={{0,16},{4,20},{8,24},{12,28},{16,0},{20,4},{24,8},{28,12},{1,17},{... | collective-permute-start | bytes 2312 | tf_op jit(solution)/shard_map/ppermute | solution.py:27
  22.6 12.0 %copy.11 = bf16[4096,1024]{1,0:T(8,128)(2,1)} copy(bf16[4096,1024]{0,1:T(8,128)(2,1)} %bitcast.45) | data formatting | bytes 16777216 | tf_op jit(solution)/shard_map/dot_general | solution.py:105
  34.9 6.0 %fusion.15 = f32[8,8,32,128]{3,1,2,0:T(8,128)S(1)} fusion(bf16[32,128,1024,1]{2,1,0,3:T(8,128)(2,1)} %bitcast.46, f32[1024]{0:T(1024)S(1)} %multiply_multiply_fusion, s32[8,8]{1,0:T(8,128)S(1)} %multiply_add_fusion, s32[1024]{0:T(1024)S(1)} %bitcast.54), kind=kOutput, calls=%fused_computation.21 | convolution fusion | flops 537001984 | bytes 9445632 | tf_op jit(solution)/shard_map/dot_general | solution.py:105
  41.2 1.9 %collective-permute-done.5 = f32[129,8,128]{2,1,0:T(8,128)S(1)} collective-permute-done((f32[129,8,128]{2,1,0:T(8,128)S(1)}, f32[129,8,128]{2,1,0:T(8,128)S(1)}, u32[]{:S(2)}, u32[]{:S(2)}) %collective-permute-start.5) | collective-permute-done | bytes 528416 | tf_op jit(solution)/shard_map/ppermute | solution.py:27
  43.9 7.9 %collective-permute-done.6 = f32[65,8,128]{2,1,0:T(8,128)S(1)} collective-permute-done((f32[65,8,128]{2,1,0:T(8,128)S(1)}, f32[65,8,128]{2,1,0:T(8,128)S(1)}, u32[]{:S(2)}, u32[]{:S(2)}) %collective-permute-start.6) | collective-permute-done | bytes 266272 | tf_op jit(solution)/shard_map/ppermute | solution.py:27
  52.0 1.6 %collective-permute-start.7 = (f32[33,8,128]{2,1,0:T(8,128)S(1)}, f32[33,8,128]{2,1,0:T(8,128)S(1)}, u32[]{:S(2)}, u32[]{:S(2)}) collective-permute-start(f32[33,8,128]{2,1,0:T(8,128)S(1)} %pad_maximum_fusion.1), channel_id=1, source_target_pairs={{0,4},{4,0},{8,12},{12,8},{16,20},{20,16},{24,28},{28,24},{1,5},{5... | collective-permute-start | bytes 405512 | tf_op jit(solution)/shard_map/ppermute | solution.py:27
  53.5 3.5 %collective-permute-done.7 = f32[33,8,128]{2,1,0:T(8,128)S(1)} collective-permute-done((f32[33,8,128]{2,1,0:T(8,128)S(1)}, f32[33,8,128]{2,1,0:T(8,128)S(1)}, u32[]{:S(2)}, u32[]{:S(2)}) %collective-permute-start.7) | collective-permute-done | bytes 135200 | tf_op jit(solution)/shard_map/ppermute | solution.py:27
  57.1 1.4 %collective-permute-start.10 = (f32[9,8,128]{2,1,0:T(8,128)S(1)}, f32[9,8,128]{2,1,0:T(8,128)S(1)}, u32[]{:S(2)}, u32[]{:S(2)}) collective-permute-start(f32[9,8,128]{2,1,0:T(8,128)S(1)} %get-tuple-element.27), channel_id=1, source_target_pairs={{0,24},{4,28},{8,0},{12,4},{16,8},{20,12},{24,16},{28,20},{1,25},{... | collective-permute-start | bytes 110600 | tf_op jit(solution)/shard_map/ppermute | solution.py:27
  59.2 1.0 %collective-permute-start.9 = (f32[9,8,128]{2,1,0:T(8,128)S(1)}, f32[9,8,128]{2,1,0:T(8,128)S(1)}, u32[]{:S(2)}, u32[]{:S(2)}) collective-permute-start(f32[9,8,128]{2,1,0:T(8,128)S(1)} %get-tuple-element.26), channel_id=1, source_target_pairs={{0,16},{4,20},{8,24},{12,28},{16,0},{20,4},{24,8},{28,12},{1,17},{... | collective-permute-start | bytes 110600 | tf_op jit(solution)/shard_map/ppermute | solution.py:27
  60.2 1.3 %collective-permute-done.10 = f32[9,8,128]{2,1,0:T(8,128)S(1)} collective-permute-done((f32[9,8,128]{2,1,0:T(8,128)S(1)}, f32[9,8,128]{2,1,0:T(8,128)S(1)}, u32[]{:S(2)}, u32[]{:S(2)}) %collective-permute-start.10) | collective-permute-done | bytes 36896 | tf_op jit(solution)/shard_map/ppermute | solution.py:27
  61.5 2.9 %collective-permute-done.8 = f32[9,8,128]{2,1,0:T(8,128)S(1)} collective-permute-done((f32[9,8,128]{2,1,0:T(8,128)S(1)}, f32[9,8,128]{2,1,0:T(8,128)S(1)}, u32[]{:S(2)}, u32[]{:S(2)}) %collective-permute-start.8) | collective-permute-done | bytes 36896 | tf_op jit(solution)/shard_map/ppermute | solution.py:27
  64.5 1.2 %collective-permute-start.11 = (f32[8,8,128]{2,1,0:T(8,128)S(1)}, f32[8,8,128]{2,1,0:T(8,128)S(1)}, u32[]{:S(2)}, u32[]{:S(2)}) collective-permute-start(f32[8,8,128]{2,1,0:T(8,128)S(1)} %get-tuple-element.19), channel_id=1, source_target_pairs={{0,8},{4,12},{8,16},{12,20},{16,24},{20,28},{24,0},{28,4},{1,9},{5... | collective-permute-start | bytes 98312 | tf_op jit(solution)/shard_map/ppermute | solution.py:27
  65.7 2.1 %collective-permute-start.12 = (f32[8,8,128]{2,1,0:T(8,128)S(1)}, f32[8,8,128]{2,1,0:T(8,128)S(1)}, u32[]{:S(2)}, u32[]{:S(2)}) collective-permute-start(f32[8,8,128]{2,1,0:T(8,128)S(1)} %get-tuple-element.19), channel_id=1, source_target_pairs={{0,16},{4,20},{8,24},{12,28},{16,0},{20,4},{24,8},{28,12},{1,17},{... | collective-permute-start | bytes 98312 | tf_op jit(solution)/shard_map/ppermute | solution.py:27
  68.4 1.9 %collective-permute-done.11 = f32[8,8,128]{2,1,0:T(8,128)S(1)} collective-permute-done((f32[8,8,128]{2,1,0:T(8,128)S(1)}, f32[8,8,128]{2,1,0:T(8,128)S(1)}, u32[]{:S(2)}, u32[]{:S(2)}) %collective-permute-start.11) | collective-permute-done | bytes 32800 | tf_op jit(solution)/shard_map/ppermute | solution.py:27
  71.8 1.5 %collective-permute-start.14 = (f32[32,8,128]{2,1,0:T(8,128)S(1)}, f32[32,8,128]{2,1,0:T(8,128)S(1)}, u32[]{:S(2)}, u32[]{:S(2)}) collective-permute-start(f32[32,8,128]{2,1,0:T(8,128)S(1)} %constant_dynamic-update-slice_fusion.6), channel_id=1, source_target_pairs={{0,4},{4,0},{8,12},{12,8},{16,20},{20,16},{24,28},{28,24},{1,5},{5... | collective-permute-start | bytes 393224 | tf_op jit(solution)/shard_map/ppermute | solution.py:27
  73.3 3.4 %collective-permute-done.14 = f32[32,8,128]{2,1,0:T(8,128)S(1)} collective-permute-done((f32[32,8,128]{2,1,0:T(8,128)S(1)}, f32[32,8,128]{2,1,0:T(8,128)S(1)}, u32[]{:S(2)}, u32[]{:S(2)}) %collective-permute-start.14) | collective-permute-done | bytes 131104 | tf_op jit(solution)/shard_map/ppermute | solution.py:27
  77.4 5.8 %collective-permute-done.15 = f32[64,8,128]{2,1,0:T(8,128)S(1)} collective-permute-done((f32[64,8,128]{2,1,0:T(8,128)S(1)}, f32[64,8,128]{2,1,0:T(8,128)S(1)}, u32[]{:S(2)}, u32[]{:S(2)}) %collective-permute-start.15) | collective-permute-done | bytes 262176 | tf_op jit(solution)/shard_map/ppermute | solution.py:27
  84.0 1.2 %collective-permute-done.16 = f32[128,8,128]{2,1,0:T(8,128)S(1)} collective-permute-done((f32[128,8,128]{2,1,0:T(8,128)S(1)}, f32[128,8,128]{2,1,0:T(8,128)S(1)}, u32[]{:S(2)}, u32[]{:S(2)}) %collective-permute-start.16) | collective-permute-done | bytes 524320 | tf_op jit(solution)/shard_map/ppermute | solution.py:27
  (68 shorter events, 9.7 us)
Async XLA Ops:
  0.6 6.0 %copy-start = (bf16[4096,64]{0,1:T(8,128)(2,1)S(1)}, bf16[4096,64]{0,1:T(8,128)(2,1)}, u32[]{:S(2)}) copy-start(bf16[4096,64]{0,1:T(8,128)(2,1)} %param.9) | copy-start | bytes 1572868
  2.3 1.4 %collective-permute-start = (f32[3,64]{1,0:T(4,128)S(1)}, f32[3,64]{1,0:T(4,128)S(1)}, u32[]{:S(2)}, u32[]{:S(2)}) collective-permute-start(f32[3,64]{1,0:T(4,128)S(1)} %pad_maximum_fusion.5), channel_id=1, source_target_pairs={{0,1},{1,0},{2,3},{3,2},{4,5},{5,4},{6,7},{7,6},{8,9},{9,8},{10,11... | collective-permute-start | bytes 2312 | tf_op jit(solution)/shard_map/ppermute | solution.py:27
  3.7 9.0 %collective-permute-start.1 = (f32[3,64]{1,0:T(4,128)S(1)}, f32[3,64]{1,0:T(4,128)S(1)}, u32[]{:S(2)}, u32[]{:S(2)}) collective-permute-start(f32[3,64]{1,0:T(4,128)S(1)} %fusion.22), channel_id=1, source_target_pairs={{0,2},{1,3},{2,0},{3,1},{4,6},{5,7},{6,4},{7,5},{8,10},{9,11},{10,... | collective-permute-start | bytes 2312 | tf_op jit(solution)/shard_map/ppermute | solution.py:27
  12.7 3.7 %collective-permute-start.2 = (f32[3,64]{1,0:T(4,128)S(1)}, f32[3,64]{1,0:T(4,128)S(1)}, u32[]{:S(2)}, u32[]{:S(2)}) collective-permute-start(f32[3,64]{1,0:T(4,128)S(1)} %fusion.25), channel_id=1, source_target_pairs={{0,4},{4,0},{8,12},{12,8},{16,20},{20,16},{24,28},{28,24},{1,5},{5... | collective-permute-start | bytes 2312 | tf_op jit(solution)/shard_map/ppermute | solution.py:27
  16.4 3.6 %collective-permute-start.3 = (f32[3,64]{1,0:T(4,128)S(1)}, f32[3,64]{1,0:T(4,128)S(1)}, u32[]{:S(2)}, u32[]{:S(2)}) collective-permute-start(f32[3,64]{1,0:T(4,128)S(1)} %add.210), channel_id=1, source_target_pairs={{0,8},{4,12},{8,0},{12,4},{16,24},{20,28},{24,16},{28,20},{1,9},{5... | collective-permute-start | bytes 2312 | tf_op jit(solution)/shard_map/ppermute | solution.py:27
  20.0 14.6 %collective-permute-start.4 = (f32[3,64]{1,0:T(4,128)S(1)}, f32[3,64]{1,0:T(4,128)S(1)}, u32[]{:S(2)}, u32[]{:S(2)}) collective-permute-start(f32[3,64]{1,0:T(4,128)S(1)} %add.211), channel_id=1, source_target_pairs={{0,16},{4,20},{8,24},{12,28},{16,0},{20,4},{24,8},{28,12},{1,17},{... | collective-permute-start | bytes 2312 | tf_op jit(solution)/shard_map/ppermute | solution.py:27
  22.6 12.0 %copy-start.2 = (s32[1,1024]{1,0:T(1,128)S(1)}, s32[1,1024]{1,0:T(1,128)}, u32[]{:S(2)}) copy-start(s32[1,1024]{1,0:T(1,128)} %param.12) | copy-start | bytes 12292
  22.6 12.1 %copy-start.3 = (f32[1,1024]{1,0:T(1,128)S(1)}, f32[1,1024]{1,0:T(1,128)}, u32[]{:S(2)}) copy-start(f32[1,1024]{1,0:T(1,128)} %param.11) | copy-start | bytes 12292
  34.8 6.2 %copy-start.4 = (f32[1024]{0:T(1024)}, f32[1024]{0:T(1024)S(1)}, u32[]{:S(2)}) copy-start(f32[1024]{0:T(1024)S(1)} %select_reduce_fusion.2) | copy-start | bytes 12292
  41.0 2.0 %collective-permute-start.5 = (f32[129,8,128]{2,1,0:T(8,128)S(1)}, f32[129,8,128]{2,1,0:T(8,128)S(1)}, u32[]{:S(2)}, u32[]{:S(2)}) collective-permute-start(f32[129,8,128]{2,1,0:T(8,128)S(1)} %select_maximum_fusion), channel_id=1, source_target_pairs={{0,1},{1,0},{2,3},{3,2},{4,5},{5,4},{6,7},{7,6},{8,9},{9,8},{10,11... | collective-permute-start | bytes 1585160 | tf_op jit(solution)/shard_map/ppermute | solution.py:27
  43.4 8.5 %collective-permute-start.6 = (f32[65,8,128]{2,1,0:T(8,128)S(1)}, f32[65,8,128]{2,1,0:T(8,128)S(1)}, u32[]{:S(2)}, u32[]{:S(2)}) collective-permute-start(f32[65,8,128]{2,1,0:T(8,128)S(1)} %pad_maximum_fusion), channel_id=1, source_target_pairs={{0,2},{1,3},{2,0},{3,1},{4,6},{5,7},{6,4},{7,5},{8,10},{9,11},{10,... | collective-permute-start | bytes 798728 | tf_op jit(solution)/shard_map/ppermute | solution.py:27
  52.0 5.1 %collective-permute-start.7 = (f32[33,8,128]{2,1,0:T(8,128)S(1)}, f32[33,8,128]{2,1,0:T(8,128)S(1)}, u32[]{:S(2)}, u32[]{:S(2)}) collective-permute-start(f32[33,8,128]{2,1,0:T(8,128)S(1)} %pad_maximum_fusion.1), channel_id=1, source_target_pairs={{0,4},{4,0},{8,12},{12,8},{16,20},{20,16},{24,28},{28,24},{1,5},{5... | collective-permute-start | bytes 405512 | tf_op jit(solution)/shard_map/ppermute | solution.py:27
  57.1 4.4 %collective-permute-start.10 = (f32[9,8,128]{2,1,0:T(8,128)S(1)}, f32[9,8,128]{2,1,0:T(8,128)S(1)}, u32[]{:S(2)}, u32[]{:S(2)}) collective-permute-start(f32[9,8,128]{2,1,0:T(8,128)S(1)} %get-tuple-element.27), channel_id=1, source_target_pairs={{0,24},{4,28},{8,0},{12,4},{16,8},{20,12},{24,16},{28,20},{1,25},{... | collective-permute-start | bytes 110600 | tf_op jit(solution)/shard_map/ppermute | solution.py:27
  58.5 5.9 %collective-permute-start.8 = (f32[9,8,128]{2,1,0:T(8,128)S(1)}, f32[9,8,128]{2,1,0:T(8,128)S(1)}, u32[]{:S(2)}, u32[]{:S(2)}) collective-permute-start(f32[9,8,128]{2,1,0:T(8,128)S(1)} %get-tuple-element.25), channel_id=1, source_target_pairs={{0,8},{4,12},{8,16},{12,20},{16,24},{20,28},{24,0},{28,4},{1,9},{5... | collective-permute-start | bytes 110600 | tf_op jit(solution)/shard_map/ppermute | solution.py:27
  59.2 5.3 %collective-permute-start.9 = (f32[9,8,128]{2,1,0:T(8,128)S(1)}, f32[9,8,128]{2,1,0:T(8,128)S(1)}, u32[]{:S(2)}, u32[]{:S(2)}) collective-permute-start(f32[9,8,128]{2,1,0:T(8,128)S(1)} %get-tuple-element.26), channel_id=1, source_target_pairs={{0,16},{4,20},{8,24},{12,28},{16,0},{20,4},{24,8},{28,12},{1,17},{... | collective-permute-start | bytes 110600 | tf_op jit(solution)/shard_map/ppermute | solution.py:27
  64.5 5.8 %collective-permute-start.11 = (f32[8,8,128]{2,1,0:T(8,128)S(1)}, f32[8,8,128]{2,1,0:T(8,128)S(1)}, u32[]{:S(2)}, u32[]{:S(2)}) collective-permute-start(f32[8,8,128]{2,1,0:T(8,128)S(1)} %get-tuple-element.19), channel_id=1, source_target_pairs={{0,8},{4,12},{8,16},{12,20},{16,24},{20,28},{24,0},{28,4},{1,9},{5... | collective-permute-start | bytes 98312 | tf_op jit(solution)/shard_map/ppermute | solution.py:27
  65.7 5.2 %collective-permute-start.12 = (f32[8,8,128]{2,1,0:T(8,128)S(1)}, f32[8,8,128]{2,1,0:T(8,128)S(1)}, u32[]{:S(2)}, u32[]{:S(2)}) collective-permute-start(f32[8,8,128]{2,1,0:T(8,128)S(1)} %get-tuple-element.19), channel_id=1, source_target_pairs={{0,16},{4,20},{8,24},{12,28},{16,0},{20,4},{24,8},{28,12},{1,17},{... | collective-permute-start | bytes 98312 | tf_op jit(solution)/shard_map/ppermute | solution.py:27
  67.9 3.9 %collective-permute-start.13 = (f32[8,8,128]{2,1,0:T(8,128)S(1)}, f32[8,8,128]{2,1,0:T(8,128)S(1)}, u32[]{:S(2)}, u32[]{:S(2)}) collective-permute-start(f32[8,8,128]{2,1,0:T(8,128)S(1)} %get-tuple-element.19), channel_id=1, source_target_pairs={{0,24},{4,28},{8,0},{12,4},{16,8},{20,12},{24,16},{28,20},{1,25},{... | collective-permute-start | bytes 98312 | tf_op jit(solution)/shard_map/ppermute | solution.py:27
  71.8 5.0 %collective-permute-start.14 = (f32[32,8,128]{2,1,0:T(8,128)S(1)}, f32[32,8,128]{2,1,0:T(8,128)S(1)}, u32[]{:S(2)}, u32[]{:S(2)}) collective-permute-start(f32[32,8,128]{2,1,0:T(8,128)S(1)} %constant_dynamic-update-slice_fusion.6), channel_id=1, source_target_pairs={{0,4},{4,0},{8,12},{12,8},{16,20},{20,16},{24,28},{28,24},{1,5},{5... | collective-permute-start | bytes 393224 | tf_op jit(solution)/shard_map/ppermute | solution.py:27
  76.8 6.4 %collective-permute-start.15 = (f32[64,8,128]{2,1,0:T(8,128)S(1)}, f32[64,8,128]{2,1,0:T(8,128)S(1)}, u32[]{:S(2)}, u32[]{:S(2)}) collective-permute-start(f32[64,8,128]{2,1,0:T(8,128)S(1)} %constant_dynamic-update-slice_fusion.4), channel_id=1, source_target_pairs={{0,2},{1,3},{2,0},{3,1},{4,6},{5,7},{6,4},{7,5},{8,10},{9,11},{10,... | collective-permute-start | bytes 786440 | tf_op jit(solution)/shard_map/ppermute | solution.py:27
  83.2 2.0 %collective-permute-start.16 = (f32[128,8,128]{2,1,0:T(8,128)S(1)}, f32[128,8,128]{2,1,0:T(8,128)S(1)}, u32[]{:S(2)}, u32[]{:S(2)}) collective-permute-start(f32[128,8,128]{2,1,0:T(8,128)S(1)} %constant_dynamic-update-slice_fusion.2), channel_id=1, source_target_pairs={{0,1},{1,0},{2,3},{3,2},{4,5},{5,4},{6,7},{7,6},{8,9},{9,8},{10,11... | collective-permute-start | bytes 1572872 | tf_op jit(solution)/shard_map/ppermute | solution.py:27
  85.2 1.0 %copy-start.1 = (f32[256,8,128]{2,1,0:T(8,128)}, f32[256,8,128]{2,1,0:T(8,128)S(1)}, u32[]{:S(2)}) copy-start(f32[256,8,128]{2,1,0:T(8,128)S(1)} %constant_dynamic-update-slice_fusion) | copy-start | bytes 3145732

commit v2 on v1

v2 whole, which is shorter than its diff:
```python
import jax
import jax.numpy as jnp
from jax import lax
from jax.sharding import PartitionSpec as P

LANES = 128
SUBLANES = 8
AXES = ("dp", "seq")


def factor(left, widest):
    return next(r for r in [widest, 2] + list(range(3, left + 1)) if left % r == 0)


def small_rounds(total):
    rounds, stride = [], 1
    while stride < total:
        radix = factor(total // stride, 2)
        rounds.append((stride, radix))
        stride *= radix
    return rounds


def wide_rounds(dp, seq):
    rounds = []
    for first, left, plan in ((1, seq, (2, 2)), (seq, dp, (2, 4))):
        stride, at = first, 0
        while left > 1:
            radix = factor(left, plan[min(at, 1)])
            rounds.append((stride, radix))
            stride, left, at = stride * radix, left // radix, at + 1
    paired = [((stride, stride), radix) for stride, radix in rounds]
    ahead = [at for at, (stride, radix) in enumerate(rounds) if stride == seq]
    if len(rounds) > 2 and rounds[0] == (1, 2) and seq > 2 and ahead:
        one, other = rounds[1], rounds[ahead[0]]
        if one[1] == other[1] and one[0] != other[0]:
            paired[1] = ((one[0], other[0]), one[1])
            paired[ahead[0]] = ((other[0], one[0]), one[1])
            paired.insert(2, paired.pop(ahead[0]))
    return paired


def shift(value, strides, radix, by):
    pairs = []
    for source in range(lax.axis_size(AXES)):
        stride = strides[source % 2]
        digit = (source // stride) % radix
        pairs.append((source, source + ((digit + by) % radix - digit) * stride))
    return lax.ppermute(value, AXES, pairs)


def digit_of(strides, radix):
    here = lax.axis_index(AXES)
    stride = jnp.where(here % 2 == 0, strides[0], strides[1])
    return (here // stride) % radix


def scatter_sum(tiles, extra, rounds):
    for strides, radix in rounds:
        mine = digit_of(strides, radix)
        count = tiles.shape[0] // radix
        got = []
        for by in range(1, radix):
            part = lax.dynamic_slice_in_dim(tiles, ((mine + by) % radix) * count, count, 0)
            got.append(shift(jnp.concatenate([part, extra], axis=0), strides, radix, by))
        tiles = lax.dynamic_slice_in_dim(tiles, mine * count, count, 0)
        for piece in got:
            tiles = tiles + piece[:count]
            extra = extra + piece[count:]
    return tiles, extra


def gather(tiles, rounds):
    for strides, radix in reversed(rounds):
        mine = digit_of(strides, radix)
        count = tiles.shape[0]
        got = [shift(tiles, strides, radix, by) for by in range(1, radix)]
        whole = jnp.zeros((count * radix,) + tiles.shape[1:], tiles.dtype)
        whole = lax.dynamic_update_slice_in_dim(whole, tiles, mine * count, 0)
        for by in range(1, radix):
            whole = lax.dynamic_update_slice_in_dim(whole, got[by - 1], ((mine - by) % radix) * count, 0)
        tiles = whole
    return tiles


def on_device(hidden, value_weight, value_bias, returns, task_bins, loss_mask):
    dp, seq = lax.axis_size("dp"), lax.axis_size("seq")
    rounds = wide_rounds(dp, seq)
    rollouts = hidden.shape[0] * dp
    width, tasks = value_weight.shape
    states = hidden.reshape(-1, width)
    flat_returns = returns.reshape(-1)
    bins = task_bins.reshape(-1)
    bins_iota = jnp.arange(tasks, dtype=jnp.int32)
    onehot = (bins[:, None] == bins_iota) & (loss_mask.reshape(-1)[:, None] != 0)
    counts = jnp.sum(jnp.where(onehot, 1.0, 0.0), axis=0)
    summed = jnp.sum(jnp.where(onehot, flat_returns[:, None], 0.0), axis=0)
    squares = jnp.sum(jnp.where(onehot, flat_returns[:, None] * flat_returns[:, None], 0.0), axis=0)
    stats = jnp.stack([counts, summed, squares])
    chosen = (bins[:, None] == bins_iota).astype(jnp.float32)
    half = states.shape[0] // 2
    pieces = []
    for at, (stride, radix) in enumerate(small_rounds(dp * seq)):
        got = [shift(stats, (stride, stride), radix, by) for by in range(1, radix)]
        if at in (1, 2):
            rows = slice(0, half) if at == 1 else slice(half, None)
            bias, stats = lax.optimization_barrier((value_bias, stats))
            scores = jnp.dot(states[rows], value_weight, preferred_element_type=jnp.float32)
            picked = jnp.sum((scores + bias) * chosen[rows], axis=-1)
            got, picked = lax.optimization_barrier((got, picked))
            pieces.append(picked)
        for piece in got:
            stats = stats + piece
    predicted = jnp.concatenate(pieces)
    counts, summed, squares = stats
    floor_counts = jnp.maximum(counts, 1.0)
    means = summed / floor_counts
    second = squares - summed * means
    spread = jnp.sqrt(second / floor_counts + 0.1)
    deviation = flat_returns[:, None] - means
    targets = jnp.sum(chosen * (deviation / spread), axis=-1)
    valid = loss_mask.reshape(-1).astype(jnp.float32)
    slope = valid * jnp.clip(predicted - targets, -1.0, 1.0) / rollouts
    coefficient = chosen * slope[:, None]
    weight_grad = lax.dot_general(
        states,
        coefficient.astype(jnp.bfloat16),
        (((0,), (0,)), ((), ())),
        preferred_element_type=jnp.float32,
    )
    weight_grad = lax.optimization_barrier(weight_grad).T
    bias_grad = jnp.sum(coefficient, axis=0)
    up, across = tasks // SUBLANES, width // LANES
    tiles = weight_grad.reshape(up, SUBLANES, across, LANES).transpose(0, 2, 1, 3)
    tiles = tiles.reshape(up * across, SUBLANES, LANES)
    extra = jnp.zeros((SUBLANES, LANES), jnp.float32).at[0, :tasks].set(bias_grad)[None]
    tiles, extra = scatter_sum(tiles, extra, rounds)
    tiles = gather(tiles, rounds)
    weight_grad = tiles.reshape(up, across, SUBLANES, LANES).transpose(0, 2, 1, 3)
    weight_grad = weight_grad.reshape(tasks, width).T
    return (targets.reshape(returns.shape), weight_grad, extra[0, 0, :tasks])


def solution(mesh):
    placed = (P("dp", "seq", None), P(), P(), P("dp", "seq"), P("dp", "seq"), P("dp", "seq"))
    return jax.shard_map(
        on_device, mesh=mesh, in_specs=placed, out_specs=(P("dp", "seq"), P(), P()), check_vma=False
    )
```

time: 86.7 us -> 76.2 us (0.88)
  local copies, waits for them, and re-layouts: 14.1 us -> 2.1 us
  other arithmetic: 2.2 us -> 3.66 us
    dot_general x1 -> x0, local copies, waits for them, and re-layouts: 12 us -> none  [on_device(): lax.dot_general(coefficient.astype(jnp.bfloat16), states, (((0,), (0,)),...]
    dot_general x2 -> x3, matrix products: 12.1 us -> 12.1 us  [the longest x2 7.19 us: on_device(): jnp.dot(states[rows], value_weight, preferred_element_type=jnp.float32)]
  transfers between devices with their start and end apart: 17 -> 17, of which waited for: 15 -> 14; matrix products, arithmetic and copies ran while one was open for 22% -> 11% of each run, Pallas kernels for 0% -> 0%
where the time goes in v2:
time: 76.2 us; the launch traced here: 75.9 us
  waiting for transfers between devices  36.7 us (48%)
  starting transfers between devices  20.2 us (27%)
  matrix products  12.1 us (16%)
  other arithmetic  3.66 us (5%)
  local copies, waits for them, and re-layouts  2.1 us (3%)
  between operations  1.05 us (1%)
    ppermute x17, waiting for transfers between devices, shift(): return lax.ppermute(value, AXES, pairs)  36.7 us
    ppermute x17, starting transfers between devices, shift(): return lax.ppermute(value, AXES, pairs)  20.2 us
    dot_general x2, matrix products, on_device(): jnp.dot(states[rows], value_weight, preferred_element_type=jnp.float32)  7.19 us
    dot_general x1, matrix products, on_device(): lax.dot_general(states, coefficient.astype(jnp.bfloat16), (((0,), (0,)),...  4.95 us
  transfers between devices with their start and end apart: 17, of which 14 were waited for; matrix products, arithmetic and copies ran while one was open for 11% of the time, Pallas kernels for 0%

profile of v2, /device:TPU:0, one launch (start us, length us, event | category | flops | bytes accessed | tf_op | source)
XLA Modules:
  0.0 75.9 jit_solution(4711212764856354755)
XLA Ops:
  2.2 0.9 %select_reduce_fusion.4 = (f32[64]{0:T(128)S(1)}, f32[64]{0:T(128)S(1)}, f32[64]{0:T(128)S(1)}) fusion(s32[1024]{0:T(1024)} %bitcast.54, pred[1024]{0:T(1024)(128)(4,1)S(1)} %compare_reduce_fusion, f32[1024]{0:T(1024)S(1)} %mul.98, f32[1024]{0:T(1024)} %bitcast.61), kind=kLoop, calls=%fused_computation.22 | loop fusion | flops 524096 | bytes 14080 | tf_op jit(solution)/shard_map/reduce_sum | solution.py:96
  4.5 2.9 %collective-permute-start.1 = (f32[3,64]{1,0:T(4,128)S(1)}, f32[3,64]{1,0:T(4,128)S(1)}, u32[]{:S(2)}, u32[]{:S(2)}) collective-permute-start(f32[3,64]{1,0:T(4,128)S(1)} %fusion.30), channel_id=1, source_target_pairs={{0,2},{1,3},{2,0},{3,1},{4,6},{5,7},{6,4},{7,5},{8,10},{9,11},{10,... | collective-permute-start | bytes 2312 | tf_op jit(solution)/shard_map/ppermute | solution.py:49
  7.4 3.6 %fusion.22 = f32[512]{0:T(512)S(1)} fusion(f32[1024,64]{0,1:T(8,128)S(1)} %fusion.20, f32[64]{0:T(128)} %param.10, bf16[4096,64]{0,1:T(8,128)(2,1)S(1)} %copy-done, bf16[1,1024,4096]{2,1,0:T(8,128)(2,1)} %param.8), kind=kOutput, calls=%fused_computation.29 | convolution fusion | flops 268533248 | bytes 4852224 | tf_op jit(solution)/shard_map/dot_general | solution.py:108
  11.0 1.6 %collective-permute-start.2 = (f32[3,64]{1,0:T(4,128)S(1)}, f32[3,64]{1,0:T(4,128)S(1)}, u32[]{:S(2)}, u32[]{:S(2)}) collective-permute-start(f32[3,64]{1,0:T(4,128)S(1)} %add.233), channel_id=1, source_target_pairs={{0,4},{1,5},{2,6},{3,7},{4,0},{5,1},{6,2},{7,3},{8,12},{9,13},{10,... | collective-permute-start | bytes 2312 | tf_op jit(solution)/shard_map/ppermute | solution.py:49
  12.6 3.6 %fusion.17 = f32[512]{0:T(512)S(1)} fusion(bf16[4096,64]{0,1:T(8,128)(2,1)S(1)} %copy-done, bf16[1,1024,4096]{2,1,0:T(8,128)(2,1)} %param.8, f32[1024,64]{0,1:T(8,128)S(1)} %fusion.20, f32[64]{0:T(128)} %param.10), kind=kOutput, calls=%fused_computation.11 | convolution fusion | flops 268533248 | bytes 4852224 | tf_op jit(solution)/shard_map/dot_general | solution.py:108
  16.2 1.6 %collective-permute-start.3 = (f32[3,64]{1,0:T(4,128)S(1)}, f32[3,64]{1,0:T(4,128)S(1)}, u32[]{:S(2)}, u32[]{:S(2)}) collective-permute-start(f32[3,64]{1,0:T(4,128)S(1)} %add.236), channel_id=1, source_target_pairs={{0,8},{1,9},{2,10},{3,11},{4,12},{5,13},{6,14},{7,15},{8,0},{9,1},... | collective-permute-start | bytes 2312 | tf_op jit(solution)/shard_map/ppermute | solution.py:49
  17.9 2.0 %collective-permute-done.3 = f32[3,64]{1,0:T(4,128)S(1)} collective-permute-done((f32[3,64]{1,0:T(4,128)S(1)}, f32[3,64]{1,0:T(4,128)S(1)}, u32[]{:S(2)}, u32[]{:S(2)}) %collective-permute-start.3) | collective-permute-done | bytes 800 | tf_op jit(solution)/shard_map/ppermute | solution.py:49
  19.9 2.6 %collective-permute-start.4 = (f32[3,64]{1,0:T(4,128)S(1)}, f32[3,64]{1,0:T(4,128)S(1)}, u32[]{:S(2)}, u32[]{:S(2)}) collective-permute-start(f32[3,64]{1,0:T(4,128)S(1)} %add.237), channel_id=1, source_target_pairs={{0,16},{1,17},{2,18},{3,19},{4,20},{5,21},{6,22},{7,23},{8,24},{9,... | collective-permute-start | bytes 2312 | tf_op jit(solution)/shard_map/ppermute | solution.py:49
  22.5 1.9 %collective-permute-done.4 = f32[3,64]{1,0:T(4,128)S(1)} collective-permute-done((f32[3,64]{1,0:T(4,128)S(1)}, f32[3,64]{1,0:T(4,128)S(1)}, u32[]{:S(2)}, u32[]{:S(2)}) %collective-permute-start.4) | collective-permute-done | bytes 800 | tf_op jit(solution)/shard_map/ppermute | solution.py:49
  24.5 4.9 %fusion.2 = f32[4096,64]{0,1:T(8,128)S(1)} fusion(bf16[1,1024,4096]{2,1,0:T(8,128)(2,1)} %param.8, f32[1024]{0:T(1024)S(1)} %fusion.28, s32[1024]{0:T(1024)S(1)} %bitcast.57), kind=kOutput, calls=%fused_computation.2 | convolution fusion | flops 537001984 | bytes 9445376 | tf_op jit(solution)/shard_map/dot_general | solution.py:125
  29.9 1.8 %collective-permute-done.5 = f32[129,8,128]{2,1,0:T(8,128)S(1)} collective-permute-done((f32[129,8,128]{2,1,0:T(8,128)S(1)}, f32[129,8,128]{2,1,0:T(8,128)S(1)}, u32[]{:S(2)}, u32[]{:S(2)}) %collective-permute-start.5) | collective-permute-done | bytes 528416 | tf_op jit(solution)/shard_map/ppermute | solution.py:49
  32.6 5.9 %collective-permute-done.6 = f32[65,8,128]{2,1,0:T(8,128)S(1)} collective-permute-done((f32[65,8,128]{2,1,0:T(8,128)S(1)}, f32[65,8,128]{2,1,0:T(8,128)S(1)}, u32[]{:S(2)}, u32[]{:S(2)}) %collective-permute-start.6) | collective-permute-done | bytes 266272 | tf_op jit(solution)/shard_map/ppermute | solution.py:49
  39.2 4.5 %collective-permute-done.7 = f32[33,8,128]{2,1,0:T(8,128)S(1)} collective-permute-done((f32[33,8,128]{2,1,0:T(8,128)S(1)}, f32[33,8,128]{2,1,0:T(8,128)S(1)}, u32[]{:S(2)}, u32[]{:S(2)}) %collective-permute-start.7) | collective-permute-done | bytes 135200 | tf_op jit(solution)/shard_map/ppermute | solution.py:49
  43.8 3.7 %collective-permute-start.10 = (f32[9,8,128]{2,1,0:T(8,128)S(1)}, f32[9,8,128]{2,1,0:T(8,128)S(1)}, u32[]{:S(2)}, u32[]{:S(2)}) collective-permute-start(f32[9,8,128]{2,1,0:T(8,128)S(1)} %get-tuple-element.43), channel_id=1, source_target_pairs={{0,24},{1,25},{2,26},{3,27},{4,28},{5,29},{6,30},{7,31},{8,0},{9,1... | collective-permute-start | bytes 110600 | tf_op jit(solution)/shard_map/ppermute | solution.py:49
  47.4 1.0 %collective-permute-start.9 = (f32[9,8,128]{2,1,0:T(8,128)S(1)}, f32[9,8,128]{2,1,0:T(8,128)S(1)}, u32[]{:S(2)}, u32[]{:S(2)}) collective-permute-start(f32[9,8,128]{2,1,0:T(8,128)S(1)} %get-tuple-element.42), channel_id=1, source_target_pairs={{0,16},{1,17},{2,18},{3,19},{4,20},{5,21},{6,22},{7,23},{8,24},{9,... | collective-permute-start | bytes 110600 | tf_op jit(solution)/shard_map/ppermute | solution.py:49
  49.1 4.1 %collective-permute-done.8 = f32[9,8,128]{2,1,0:T(8,128)S(1)} collective-permute-done((f32[9,8,128]{2,1,0:T(8,128)S(1)}, f32[9,8,128]{2,1,0:T(8,128)S(1)}, u32[]{:S(2)}, u32[]{:S(2)}) %collective-permute-start.8) | collective-permute-done | bytes 36896 | tf_op jit(solution)/shard_map/ppermute | solution.py:49
  53.2 1.0 %collective-permute-start.11 = (f32[8,8,128]{2,1,0:T(8,128)S(1)}, f32[8,8,128]{2,1,0:T(8,128)S(1)}, u32[]{:S(2)}, u32[]{:S(2)}) collective-permute-start(f32[8,8,128]{2,1,0:T(8,128)S(1)} %get-tuple-element.35), channel_id=1, source_target_pairs={{0,8},{1,9},{2,10},{3,11},{4,12},{5,13},{6,14},{7,15},{8,16},{9,17... | collective-permute-start | bytes 98312 | tf_op jit(solution)/shard_map/ppermute | solution.py:49
  54.2 2.5 %collective-permute-start.12 = (f32[8,8,128]{2,1,0:T(8,128)S(1)}, f32[8,8,128]{2,1,0:T(8,128)S(1)}, u32[]{:S(2)}, u32[]{:S(2)}) collective-permute-start(f32[8,8,128]{2,1,0:T(8,128)S(1)} %get-tuple-element.35), channel_id=1, source_target_pairs={{0,16},{1,17},{2,18},{3,19},{4,20},{5,21},{6,22},{7,23},{8,24},{9,... | collective-permute-start | bytes 98312 | tf_op jit(solution)/shard_map/ppermute | solution.py:49
  57.1 1.9 %collective-permute-done.11 = f32[8,8,128]{2,1,0:T(8,128)S(1)} collective-permute-done((f32[8,8,128]{2,1,0:T(8,128)S(1)}, f32[8,8,128]{2,1,0:T(8,128)S(1)}, u32[]{:S(2)}, u32[]{:S(2)}) %collective-permute-start.11) | collective-permute-done | bytes 32800 | tf_op jit(solution)/shard_map/ppermute | solution.py:49
  59.7 1.0 %collective-permute-done.13 = f32[8,8,128]{2,1,0:T(8,128)S(1)} collective-permute-done((f32[8,8,128]{2,1,0:T(8,128)S(1)}, f32[8,8,128]{2,1,0:T(8,128)S(1)}, u32[]{:S(2)}, u32[]{:S(2)}) %collective-permute-start.13) | collective-permute-done | bytes 32800 | tf_op jit(solution)/shard_map/ppermute | solution.py:49
  61.3 5.2 %collective-permute-done.14 = f32[32,8,128]{2,1,0:T(8,128)S(1)} collective-permute-done((f32[32,8,128]{2,1,0:T(8,128)S(1)}, f32[32,8,128]{2,1,0:T(8,128)S(1)}, u32[]{:S(2)}, u32[]{:S(2)}) %collective-permute-start.14) | collective-permute-done | bytes 131104 | tf_op jit(solution)/shard_map/ppermute | solution.py:49
  67.1 5.8 %collective-permute-done.15 = f32[64,8,128]{2,1,0:T(8,128)S(1)} collective-permute-done((f32[64,8,128]{2,1,0:T(8,128)S(1)}, f32[64,8,128]{2,1,0:T(8,128)S(1)}, u32[]{:S(2)}, u32[]{:S(2)}) %collective-permute-start.15) | collective-permute-done | bytes 262176 | tf_op jit(solution)/shard_map/ppermute | solution.py:49
  73.6 1.2 %collective-permute-done.16 = f32[128,8,128]{2,1,0:T(8,128)S(1)} collective-permute-done((f32[128,8,128]{2,1,0:T(8,128)S(1)}, f32[128,8,128]{2,1,0:T(8,128)S(1)}, u32[]{:S(2)}, u32[]{:S(2)}) %collective-permute-start.16) | collective-permute-done | bytes 524320 | tf_op jit(solution)/shard_map/ppermute | solution.py:49
  74.9 1.0 %copy-done.1 = f32[256,8,128]{2,1,0:T(8,128)} copy-done((f32[256,8,128]{2,1,0:T(8,128)}, f32[256,8,128]{2,1,0:T(8,128)S(1)}, u32[]{:S(2)}) %copy-start.1) | copy-done | bytes 1048600
  (72 shorter events, 8.6 us)
Async XLA Ops:
  0.6 6.8 %copy-start = (bf16[4096,64]{0,1:T(8,128)(2,1)S(1)}, bf16[4096,64]{0,1:T(8,128)(2,1)}, u32[]{:S(2)}) copy-start(bf16[4096,64]{0,1:T(8,128)(2,1)} %param.9) | copy-start | bytes 1572868
  0.6 23.7 %copy-start.3 = (f32[1,1024]{1,0:T(1,128)S(1)}, f32[1,1024]{1,0:T(1,128)}, u32[]{:S(2)}) copy-start(f32[1,1024]{1,0:T(1,128)} %param.11) | copy-start | bytes 12292
  0.7 21.8 %copy-start.4 = (s32[1,1024]{1,0:T(1,128)S(1)}, s32[1,1024]{1,0:T(1,128)}, u32[]{:S(2)}) copy-start(s32[1,1024]{1,0:T(1,128)} %param.13) | copy-start | bytes 12292
  0.7 23.7 %copy-start.2 = (s32[1,1024]{1,0:T(1,128)S(1)}, s32[1,1024]{1,0:T(1,128)}, u32[]{:S(2)}) copy-start(s32[1,1024]{1,0:T(1,128)} %param.12) | copy-start | bytes 12292
  3.1 1.4 %collective-permute-start = (f32[3,64]{1,0:T(4,128)S(1)}, f32[3,64]{1,0:T(4,128)S(1)}, u32[]{:S(2)}, u32[]{:S(2)}) collective-permute-start(f32[3,64]{1,0:T(4,128)S(1)} %pad_maximum_fusion.5), channel_id=1, source_target_pairs={{0,1},{1,0},{2,3},{3,2},{4,5},{5,4},{6,7},{7,6},{8,9},{9,8},{10,11... | collective-permute-start | bytes 2312 | tf_op jit(solution)/shard_map/ppermute | solution.py:49
  4.5 6.5 %collective-permute-start.1 = (f32[3,64]{1,0:T(4,128)S(1)}, f32[3,64]{1,0:T(4,128)S(1)}, u32[]{:S(2)}, u32[]{:S(2)}) collective-permute-start(f32[3,64]{1,0:T(4,128)S(1)} %fusion.30), channel_id=1, source_target_pairs={{0,2},{1,3},{2,0},{3,1},{4,6},{5,7},{6,4},{7,5},{8,10},{9,11},{10,... | collective-permute-start | bytes 2312 | tf_op jit(solution)/shard_map/ppermute | solution.py:49
  11.0 5.2 %collective-permute-start.2 = (f32[3,64]{1,0:T(4,128)S(1)}, f32[3,64]{1,0:T(4,128)S(1)}, u32[]{:S(2)}, u32[]{:S(2)}) collective-permute-start(f32[3,64]{1,0:T(4,128)S(1)} %add.233), channel_id=1, source_target_pairs={{0,4},{1,5},{2,6},{3,7},{4,0},{5,1},{6,2},{7,3},{8,12},{9,13},{10,... | collective-permute-start | bytes 2312 | tf_op jit(solution)/shard_map/ppermute | solution.py:49
  16.2 3.7 %collective-permute-start.3 = (f32[3,64]{1,0:T(4,128)S(1)}, f32[3,64]{1,0:T(4,128)S(1)}, u32[]{:S(2)}, u32[]{:S(2)}) collective-permute-start(f32[3,64]{1,0:T(4,128)S(1)} %add.236), channel_id=1, source_target_pairs={{0,8},{1,9},{2,10},{3,11},{4,12},{5,13},{6,14},{7,15},{8,0},{9,1},... | collective-permute-start | bytes 2312 | tf_op jit(solution)/shard_map/ppermute | solution.py:49
  19.9 4.5 %collective-permute-start.4 = (f32[3,64]{1,0:T(4,128)S(1)}, f32[3,64]{1,0:T(4,128)S(1)}, u32[]{:S(2)}, u32[]{:S(2)}) collective-permute-start(f32[3,64]{1,0:T(4,128)S(1)} %add.237), channel_id=1, source_target_pairs={{0,16},{1,17},{2,18},{3,19},{4,20},{5,21},{6,22},{7,23},{8,24},{9,... | collective-permute-start | bytes 2312 | tf_op jit(solution)/shard_map/ppermute | solution.py:49
  24.5 5.2 %copy-start.5 = (f32[1024]{0:T(1024)}, f32[1024]{0:T(1024)S(1)}, u32[]{:S(2)}) copy-start(f32[1024]{0:T(1024)S(1)} %select_reduce_fusion.1) | copy-start | bytes 12292
  29.7 2.0 %collective-permute-start.5 = (f32[129,8,128]{2,1,0:T(8,128)S(1)}, f32[129,8,128]{2,1,0:T(8,128)S(1)}, u32[]{:S(2)}, u32[]{:S(2)}) collective-permute-start(f32[129,8,128]{2,1,0:T(8,128)S(1)} %select_maximum_fusion), channel_id=1, source_target_pairs={{0,1},{1,0},{2,3},{3,2},{4,5},{5,4},{6,7},{7,6},{8,9},{9,8},{10,11... | collective-permute-start | bytes 1585160 | tf_op jit(solution)/shard_map/ppermute | solution.py:49
  32.1 6.5 %collective-permute-start.6 = (f32[65,8,128]{2,1,0:T(8,128)S(1)}, f32[65,8,128]{2,1,0:T(8,128)S(1)}, u32[]{:S(2)}, u32[]{:S(2)}) collective-permute-start(f32[65,8,128]{2,1,0:T(8,128)S(1)} %pad_maximum_fusion), channel_id=1, source_target_pairs={{0,2},{1,5},{2,0},{3,7},{4,6},{5,1},{6,4},{7,3},{8,10},{9,13},{10,... | collective-permute-start | bytes 798728 | tf_op jit(solution)/shard_map/ppermute | solution.py:49
  38.6 5.1 %collective-permute-start.7 = (f32[33,8,128]{2,1,0:T(8,128)S(1)}, f32[33,8,128]{2,1,0:T(8,128)S(1)}, u32[]{:S(2)}, u32[]{:S(2)}) collective-permute-start(f32[33,8,128]{2,1,0:T(8,128)S(1)} %pad_maximum_fusion.1), channel_id=1, source_target_pairs={{0,4},{1,3},{2,6},{3,1},{4,0},{5,7},{6,2},{7,5},{8,12},{9,11},{10,... | collective-permute-start | bytes 405512 | tf_op jit(solution)/shard_map/ppermute | solution.py:49
  43.8 5.3 %collective-permute-start.10 = (f32[9,8,128]{2,1,0:T(8,128)S(1)}, f32[9,8,128]{2,1,0:T(8,128)S(1)}, u32[]{:S(2)}, u32[]{:S(2)}) collective-permute-start(f32[9,8,128]{2,1,0:T(8,128)S(1)} %get-tuple-element.43), channel_id=1, source_target_pairs={{0,24},{1,25},{2,26},{3,27},{4,28},{5,29},{6,30},{7,31},{8,0},{9,1... | collective-permute-start | bytes 110600 | tf_op jit(solution)/shard_map/ppermute | solution.py:49
  47.4 5.8 %collective-permute-start.8 = (f32[9,8,128]{2,1,0:T(8,128)S(1)}, f32[9,8,128]{2,1,0:T(8,128)S(1)}, u32[]{:S(2)}, u32[]{:S(2)}) collective-permute-start(f32[9,8,128]{2,1,0:T(8,128)S(1)} %get-tuple-element.41), channel_id=1, source_target_pairs={{0,8},{1,9},{2,10},{3,11},{4,12},{5,13},{6,14},{7,15},{8,16},{9,17... | collective-permute-start | bytes 110600 | tf_op jit(solution)/shard_map/ppermute | solution.py:49
  47.4 5.8 %collective-permute-start.9 = (f32[9,8,128]{2,1,0:T(8,128)S(1)}, f32[9,8,128]{2,1,0:T(8,128)S(1)}, u32[]{:S(2)}, u32[]{:S(2)}) collective-permute-start(f32[9,8,128]{2,1,0:T(8,128)S(1)} %get-tuple-element.42), channel_id=1, source_target_pairs={{0,16},{1,17},{2,18},{3,19},{4,20},{5,21},{6,22},{7,23},{8,24},{9,... | collective-permute-start | bytes 110600 | tf_op jit(solution)/shard_map/ppermute | solution.py:49
  53.2 5.8 %collective-permute-start.11 = (f32[8,8,128]{2,1,0:T(8,128)S(1)}, f32[8,8,128]{2,1,0:T(8,128)S(1)}, u32[]{:S(2)}, u32[]{:S(2)}) collective-permute-start(f32[8,8,128]{2,1,0:T(8,128)S(1)} %get-tuple-element.35), channel_id=1, source_target_pairs={{0,8},{1,9},{2,10},{3,11},{4,12},{5,13},{6,14},{7,15},{8,16},{9,17... | collective-permute-start | bytes 98312 | tf_op jit(solution)/shard_map/ppermute | solution.py:49
  54.2 5.5 %collective-permute-start.12 = (f32[8,8,128]{2,1,0:T(8,128)S(1)}, f32[8,8,128]{2,1,0:T(8,128)S(1)}, u32[]{:S(2)}, u32[]{:S(2)}) collective-permute-start(f32[8,8,128]{2,1,0:T(8,128)S(1)} %get-tuple-element.35), channel_id=1, source_target_pairs={{0,16},{1,17},{2,18},{3,19},{4,20},{5,21},{6,22},{7,23},{8,24},{9,... | collective-permute-start | bytes 98312 | tf_op jit(solution)/shard_map/ppermute | solution.py:49
  56.8 3.9 %collective-permute-start.13 = (f32[8,8,128]{2,1,0:T(8,128)S(1)}, f32[8,8,128]{2,1,0:T(8,128)S(1)}, u32[]{:S(2)}, u32[]{:S(2)}) collective-permute-start(f32[8,8,128]{2,1,0:T(8,128)S(1)} %get-tuple-element.35), channel_id=1, source_target_pairs={{0,24},{1,25},{2,26},{3,27},{4,28},{5,29},{6,30},{7,31},{8,0},{9,1... | collective-permute-start | bytes 98312 | tf_op jit(solution)/shard_map/ppermute | solution.py:49
  60.7 5.7 %collective-permute-start.14 = (f32[32,8,128]{2,1,0:T(8,128)S(1)}, f32[32,8,128]{2,1,0:T(8,128)S(1)}, u32[]{:S(2)}, u32[]{:S(2)}) collective-permute-start(f32[32,8,128]{2,1,0:T(8,128)S(1)} %constant_dynamic-update-slice_fusion.6), channel_id=1, source_target_pairs={{0,4},{1,3},{2,6},{3,1},{4,0},{5,7},{6,2},{7,5},{8,12},{9,11},{10,... | collective-permute-start | bytes 393224 | tf_op jit(solution)/shard_map/ppermute | solution.py:49
  66.5 6.4 %collective-permute-start.15 = (f32[64,8,128]{2,1,0:T(8,128)S(1)}, f32[64,8,128]{2,1,0:T(8,128)S(1)}, u32[]{:S(2)}, u32[]{:S(2)}) collective-permute-start(f32[64,8,128]{2,1,0:T(8,128)S(1)} %constant_dynamic-update-slice_fusion.4), channel_id=1, source_target_pairs={{0,2},{1,5},{2,0},{3,7},{4,6},{5,1},{6,4},{7,3},{8,10},{9,13},{10,... | collective-permute-start | bytes 786440 | tf_op jit(solution)/shard_map/ppermute | solution.py:49
  72.9 2.0 %collective-permute-start.16 = (f32[128,8,128]{2,1,0:T(8,128)S(1)}, f32[128,8,128]{2,1,0:T(8,128)S(1)}, u32[]{:S(2)}, u32[]{:S(2)}) collective-permute-start(f32[128,8,128]{2,1,0:T(8,128)S(1)} %constant_dynamic-update-slice_fusion.2), channel_id=1, source_target_pairs={{0,1},{1,0},{2,3},{3,2},{4,5},{5,4},{6,7},{7,6},{8,9},{9,8},{10,11... | collective-permute-start | bytes 1572872 | tf_op jit(solution)/shard_map/ppermute | solution.py:49
  74.9 1.0 %copy-start.1 = (f32[256,8,128]{2,1,0:T(8,128)}, f32[256,8,128]{2,1,0:T(8,128)S(1)}, u32[]{:S(2)}) copy-start(f32[256,8,128]{2,1,0:T(8,128)S(1)} %constant_dynamic-update-slice_fusion) | copy-start | bytes 3145732

commit v3 on v2

v3 whole, which is shorter than its diff:
```python
import jax
import jax.numpy as jnp
from jax import lax
from jax.experimental import pallas as pl
from jax.sharding import PartitionSpec as P

LANES = 128
SUBLANES = 8
AXES = ("dp", "seq")


def factor(left, widest):
    return next(r for r in [widest, 2] + list(range(3, left + 1)) if left % r == 0)


def small_rounds(total):
    rounds, stride = [], 1
    while stride < total:
        radix = factor(total // stride, 2)
        rounds.append((stride, radix))
        stride *= radix
    return rounds


def wide_rounds(dp, seq):
    rounds = []
    for first, left, plan in ((1, seq, (2, 2)), (seq, dp, (2, 4))):
        stride, at = first, 0
        while left > 1:
            radix = factor(left, plan[min(at, 1)])
            rounds.append((stride, radix))
            stride, left, at = stride * radix, left // radix, at + 1
    paired = [((stride, stride), radix) for stride, radix in rounds]
    ahead = [at for at, (stride, radix) in enumerate(rounds) if stride == seq]
    if len(rounds) > 2 and rounds[0] == (1, 2) and seq > 2 and ahead:
        one, other = rounds[1], rounds[ahead[0]]
        if one[1] == other[1] and one[0] != other[0]:
            paired[1] = ((one[0], other[0]), one[1])
            paired[ahead[0]] = ((other[0], one[0]), one[1])
            paired.insert(2, paired.pop(ahead[0]))
    return paired


def shift(value, strides, radix, by):
    pairs = []
    for source in range(lax.axis_size(AXES)):
        stride = strides[source % 2]
        digit = (source // stride) % radix
        pairs.append((source, source + ((digit + by) % radix - digit) * stride))
    return lax.ppermute(value, AXES, pairs)


def digit_of(strides, radix):
    here = lax.axis_index(AXES)
    stride = jnp.where(here % 2 == 0, strides[0], strides[1])
    return (here // stride) % radix


def scatter_round(tiles, extra, strides, radix):
    mine = digit_of(strides, radix)
    count = tiles.shape[0] // radix
    got = []
    for by in range(1, radix):
        part = lax.dynamic_slice_in_dim(tiles, ((mine + by) % radix) * count, count, 0)
        part = part if extra is None else jnp.concatenate([part, extra], axis=0)
        got.append(shift(part, strides, radix, by))
    tiles = lax.dynamic_slice_in_dim(tiles, mine * count, count, 0)
    for piece in got:
        tiles = tiles + piece[:count]
        extra = None if extra is None else extra + piece[count:]
    return tiles, extra


def gather_round(tiles, strides, radix):
    mine = digit_of(strides, radix)
    count = tiles.shape[0]
    got = [shift(tiles, strides, radix, by) for by in range(1, radix)]
    whole = jnp.zeros((count * radix,) + tiles.shape[1:], tiles.dtype)
    whole = lax.dynamic_update_slice_in_dim(whole, tiles, mine * count, 0)
    for by in range(1, radix):
        whole = lax.dynamic_update_slice_in_dim(whole, got[by - 1], ((mine - by) % radix) * count, 0)
    return whole


def all_sum(chains, extra, rounds):
    apart = min(3, len(rounds)) if len(chains) > 1 else 0
    extras = [None] * (len(chains) - 1) + [extra]
    for strides, radix in rounds[:apart]:
        both = [scatter_round(tiles, more, strides, radix) for tiles, more in zip(chains, extras)]
        chains, extras = [one[0] for one in both], [one[1] for one in both]
    extra = extras[-1]
    count = chains[0].shape[0]
    tiles = jnp.concatenate(chains, axis=0)
    for strides, radix in rounds[apart:]:
        tiles, extra = scatter_round(tiles, extra, strides, radix)
    for strides, radix in reversed(rounds[apart:]):
        tiles = gather_round(tiles, strides, radix)
    chains = [tiles[at * count:(at + 1) * count] for at in range(len(chains))]
    for strides, radix in reversed(rounds[:apart]):
        chains = [gather_round(tiles, strides, radix) for tiles in chains]
    return chains, extra


def stats_kernel(returns_ref, bins_ref, mask_ref, out_ref):
    rows, tasks = out_ref.shape
    tokens = returns_ref.shape[1]
    value = returns_ref[...]
    task = lax.broadcasted_iota(jnp.int32, (tasks, tokens), 0)
    onehot = (task == bins_ref[...]) & (mask_ref[...] != 0)
    row = lax.broadcasted_iota(jnp.int32, (rows, tokens), 0)
    terms = jnp.where(row == 0, 1.0, jnp.where(row == 1, value, jnp.where(row == 2, value * value, 0.0)))
    out_ref[...] = lax.dot_general(
        terms,
        jnp.where(onehot, 1.0, 0.0),
        (((1,), (1,)), ((), ())),
        precision=lax.Precision.HIGHEST,
        preferred_element_type=jnp.float32,
    )


def local_stats(returns, task_bins, loss_mask, tasks):
    return pl.pallas_call(
        stats_kernel,
        out_shape=jax.ShapeDtypeStruct((SUBLANES, tasks), jnp.float32),
        name="task_stats",
    )(returns.reshape(1, -1), task_bins.reshape(1, -1), loss_mask.reshape(1, -1))


def on_device(hidden, value_weight, value_bias, returns, task_bins, loss_mask):
    dp, seq = lax.axis_size("dp"), lax.axis_size("seq")
    rounds = wide_rounds(dp, seq)
    rollouts = hidden.shape[0] * dp
    width, tasks = value_weight.shape
    states = hidden.reshape(-1, width)
    flat_returns = returns.reshape(-1)
    bins = task_bins.reshape(-1)
    bins_iota = jnp.arange(tasks, dtype=jnp.int32)
    stats = local_stats(returns, task_bins, loss_mask, tasks)
    chosen = (bins[:, None] == bins_iota).astype(jnp.float32)
    exchanges = small_rounds(dp * seq)
    parts = len(exchanges) - 1
    edges = [states.shape[0] * at // parts for at in range(parts + 1)]
    pieces = []
    for at, (stride, radix) in enumerate(exchanges):
        got = [shift(stats, (stride, stride), radix, by) for by in range(1, radix)]
        if at:
            rows = slice(edges[at - 1], edges[at])
            bias, stats = lax.optimization_barrier((value_bias, stats))
            scores = jnp.dot(states[rows], value_weight, preferred_element_type=jnp.float32)
            picked = jnp.sum((scores + bias) * chosen[rows], axis=-1)
            got, picked = lax.optimization_barrier((got, picked))
            pieces.append(picked)
        for piece in got:
            stats = stats + piece
    predicted = jnp.concatenate(pieces)
    counts, summed, squares = stats[0], stats[1], stats[2]
    floor_counts = jnp.maximum(counts, 1.0)
    means = summed / floor_counts
    second = squares - summed * means
    spread = jnp.sqrt(second / floor_counts + 0.1)
    deviation = flat_returns[:, None] - means
    targets = jnp.sum(chosen * (deviation / spread), axis=-1)
    valid = loss_mask.reshape(-1).astype(jnp.float32)
    slope = valid * jnp.clip(predicted - targets, -1.0, 1.0) / rollouts
    coefficient = chosen * slope[:, None]
    coefficient_low = coefficient.astype(jnp.bfloat16)
    bias_grad = jnp.sum(coefficient, axis=0)
    up, across = tasks // SUBLANES, width // LANES
    count = 2 if (up * across) % (2 * dp * seq) == 0 else 1
    chains = []
    for at in range(count):
        columns = slice(width * at // count, width * (at + 1) // count)
        part = lax.dot_general(
            states[:, columns],
            coefficient_low,
            (((0,), (0,)), ((), ())),
            preferred_element_type=jnp.float32,
        )
        part = lax.optimization_barrier(part).T
        part = part.reshape(up, SUBLANES, across // count, LANES).transpose(0, 2, 1, 3)
        chains.append(part.reshape(-1, SUBLANES, LANES))
    extra = jnp.zeros((SUBLANES, LANES), jnp.float32).at[0, :tasks].set(bias_grad)[None]
    chains, extra = all_sum(chains, extra, rounds)
    whole = []
    for tiles in chains:
        part = tiles.reshape(up, across // count, SUBLANES, LANES).transpose(0, 2, 1, 3)
        whole.append(part.reshape(tasks, width // count).T)
    return (targets.reshape(returns.shape), jnp.concatenate(whole, axis=0), extra[0, 0, :tasks])


def solution(mesh):
    placed = (P("dp", "seq", None), P(), P(), P("dp", "seq"), P("dp", "seq"), P("dp", "seq"))
    return jax.shard_map(
        on_device, mesh=mesh, in_specs=placed, out_specs=(P("dp", "seq"), P(), P()), check_vma=False
    )
```

time: 76.2 us -> 67.3 us (0.88)
  waiting for transfers between devices: 36.7 us -> 21.2 us
  starting transfers between devices: 20.2 us -> 28.3 us
  matrix products: 12.1 us -> 9.57 us
  Pallas kernels: 0 us -> 1.7 us
  local copies, waits for them, and re-layouts: 2.1 us -> 1.2 us
    ppermute x17 -> x23, waiting for transfers between devices: 36.7 us -> 21.2 us  [shift(): return lax.ppermute(value, AXES, pairs)]
    ppermute x17 -> x23, starting transfers between devices: 20.2 us -> 28.3 us  [shift(): return lax.ppermute(value, AXES, pairs)]
    dot_general x1 -> x2, matrix products: 4.95 us -> 1.68 us  [on_device(): lax.dot_general(states[:, columns], coefficient_low, (((0,), (0,)), ((),...]
    pallas_call x0 -> x1, Pallas kernels: none -> 1.7 us  [local_stats(): pl.pallas_call(stats_kernel, out_shape=jax.ShapeDtypeStruct((SUBLANES, ta...]
    concatenate x4 -> x6, other arithmetic: 0.08 us -> 1.17 us  [the longest x1 1.04 us: on_device(): jnp.concatenate(whole, axis=0)]
    unnamed x12, local copies, waits for them, and re-layouts: 1 us -> 0.04 us
    reduce_sum x1 -> x0, other arithmetic: 0.93 us -> none  [on_device(): counts = jnp.sum(jnp.where(onehot, 1.0, 0.0), axis=0)]
    add x5, other arithmetic: 0.03 us -> 0.86 us  [on_device(): stats = stats + piece]
  transfers between devices with their start and end apart: 17 -> 23, of which waited for: 14 -> 16; matrix products, arithmetic and copies ran while one was open for 11% -> 16% of each run, Pallas kernels for 0% -> 0%
where the time goes in v3:
time: 67.3 us; the launch traced here: 67 us
  starting transfers between devices  28.3 us (42%)
  waiting for transfers between devices  21.2 us (32%)
  matrix products  9.57 us (14%)
  other arithmetic  3.88 us (6%)
  Pallas kernels  1.7 us (3%)
  local copies, waits for them, and re-layouts  1.2 us (2%)
  between operations  1.12 us (2%)
    ppermute x23, starting transfers between devices, shift(): return lax.ppermute(value, AXES, pairs)  28.3 us
    ppermute x23, waiting for transfers between devices, shift(): return lax.ppermute(value, AXES, pairs)  21.2 us
    dot_general x4, matrix products, on_device(): jnp.dot(states[rows], value_weight, preferred_element_type=jnp.float32)  7.89 us
    pallas_call x1, Pallas kernels, local_stats(): pl.pallas_call(stats_kernel, out_shape=jax.ShapeDtypeStruct((SUBLANES, ta...  1.7 us
    dot_general x2, matrix products, on_device(): lax.dot_general(states[:, columns], coefficient_low, (((0,), (0,)), ((),...  1.68 us
  transfers between devices with their start and end apart: 23, of which 16 were waited for; matrix products, arithmetic and copies ran while one was open for 16% of the time, Pallas kernels for 0%

profile of v3, /device:TPU:0, one launch (start us, length us, event | category | flops | bytes accessed | tf_op | source)
XLA Modules:
  0.0 67.0 jit_solution(8038621018579440067)
XLA Ops:
  0.7 1.7 %task_stats.1 = f32[8,64]{1,0:T(8,128)} custom-call(f32[1,1024]{1,0:T(1,128)} %returns_ref.1, s32[1,1024]{1,0:T(1,128)} %bins_ref.1, s32[1,1024]{1,0:T(1,128)} %mask_ref.1), custom_call_target="tpu_custom_call" | custom-call | tf_op jit(solution)/shard_map/task_stats/pallas_call | solution.py:122
  5.1 2.5 %collective-permute-start.1 = (f32[8,64]{1,0:T(8,128)S(1)}, f32[8,64]{1,0:T(8,128)S(1)}, u32[]{:S(2)}, u32[]{:S(2)}) collective-permute-start(f32[8,64]{1,0:T(8,128)S(1)} %add.294), channel_id=1, source_target_pairs={{0,2},{1,3},{2,0},{3,1},{4,6},{5,7},{6,4},{7,5},{8,10},{9,11},{10,... | collective-permute-start | bytes 6152 | tf_op jit(solution)/shard_map/ppermute | solution.py:50
  7.6 2.4 %fusion.56 = f32[256]{0:T(256)S(1)} fusion(f32[1024,64]{0,1:T(8,128)S(1)} %fusion.49, f32[64]{0:T(128)} %param.10, bf16[4096,64]{0,1:T(8,128)(2,1)S(1)} %copy-done, bf16[1,1024,4096]{2,1,0:T(8,128)(2,1)} %param.8), kind=kOutput, calls=%fused_computation.57 | convolution fusion | flops 134266624 | bytes 2688512 | tf_op jit(solution)/shard_map/dot_general | solution.py:149
  10.0 1.6 %collective-permute-start.2 = (f32[8,64]{1,0:T(8,128)S(1)}, f32[8,64]{1,0:T(8,128)S(1)}, u32[]{:S(2)}, u32[]{:S(2)}) collective-permute-start(f32[8,64]{1,0:T(8,128)S(1)} %add.297), channel_id=1, source_target_pairs={{0,4},{1,5},{2,6},{3,7},{4,0},{5,1},{6,2},{7,3},{8,12},{9,13},{10,... | collective-permute-start | bytes 6152 | tf_op jit(solution)/shard_map/ppermute | solution.py:50
  11.6 2.4 %fusion.46 = f32[256]{0:T(256)S(1)} fusion(bf16[4096,64]{0,1:T(8,128)(2,1)S(1)} %copy-done, bf16[1,1024,4096]{2,1,0:T(8,128)(2,1)} %param.8, f32[1024,64]{0,1:T(8,128)S(1)} %fusion.49, f32[64]{0:T(128)} %param.10), kind=kOutput, calls=%fused_computation.26 | convolution fusion | flops 134266624 | bytes 2688512 | tf_op jit(solution)/shard_map/dot_general | solution.py:149
  14.0 1.6 %collective-permute-start.3 = (f32[8,64]{1,0:T(8,128)S(1)}, f32[8,64]{1,0:T(8,128)S(1)}, u32[]{:S(2)}, u32[]{:S(2)}) collective-permute-start(f32[8,64]{1,0:T(8,128)S(1)} %add.300), channel_id=1, source_target_pairs={{0,8},{1,9},{2,10},{3,11},{4,12},{5,13},{6,14},{7,15},{8,0},{9,1},... | collective-permute-start | bytes 6152 | tf_op jit(solution)/shard_map/ppermute | solution.py:50
  15.7 2.4 %fusion.43 = f32[256]{0:T(256)S(1)} fusion(bf16[4096,64]{0,1:T(8,128)(2,1)S(1)} %copy-done, bf16[1,1024,4096]{2,1,0:T(8,128)(2,1)} %param.8, f32[1024,64]{0,1:T(8,128)S(1)} %fusion.49, f32[64]{0:T(128)} %param.10), kind=kOutput, calls=%fused_computation.25 | convolution fusion | flops 134266624 | bytes 2688512 | tf_op jit(solution)/shard_map/dot_general | solution.py:149
  18.1 2.7 %collective-permute-start.4 = (f32[8,64]{1,0:T(8,128)S(1)}, f32[8,64]{1,0:T(8,128)S(1)}, u32[]{:S(2)}, u32[]{:S(2)}) collective-permute-start(f32[8,64]{1,0:T(8,128)S(1)} %add.303), channel_id=1, source_target_pairs={{0,16},{1,17},{2,18},{3,19},{4,20},{5,21},{6,22},{7,23},{8,24},{9,... | collective-permute-start | bytes 6152 | tf_op jit(solution)/shard_map/ppermute | solution.py:50
  28.7 2.6 %collective-permute-done.6 = f32[32,8,128]{2,1,0:T(8,128)S(1)} collective-permute-done((f32[32,8,128]{2,1,0:T(8,128)S(1)}, f32[32,8,128]{2,1,0:T(8,128)S(1)}, u32[]{:S(2)}, u32[]{:S(2)}) %collective-permute-start.6) | collective-permute-done | bytes 131104 | tf_op jit(solution)/shard_map/ppermute | solution.py:50
  31.3 1.2 %collective-permute-start.7 = (f32[16,8,128]{2,1,0:T(8,128)S(1)}, f32[16,8,128]{2,1,0:T(8,128)S(1)}, u32[]{:S(2)}, u32[]{:S(2)}) collective-permute-start(f32[16,8,128]{2,1,0:T(8,128)S(1)} %constant_dynamic-slice_fusion.3), channel_id=1, source_target_pairs={{0,4},{1,3},{2,6},{3,1},{4,0},{5,7},{6,2},{7,5},{8,12},{9,11},{10,... | collective-permute-start | bytes 196616 | tf_op jit(solution)/shard_map/ppermute | solution.py:50
  32.8 1.2 %collective-permute-start.10 = (f32[17,8,128]{2,1,0:T(8,128)S(1)}, f32[17,8,128]{2,1,0:T(8,128)S(1)}, u32[]{:S(2)}, u32[]{:S(2)}) collective-permute-start(f32[17,8,128]{2,1,0:T(8,128)S(1)} %pad_maximum_fusion.2), channel_id=1, source_target_pairs={{0,4},{1,3},{2,6},{3,1},{4,0},{5,7},{6,2},{7,5},{8,12},{9,11},{10,... | collective-permute-start | bytes 208904 | tf_op jit(solution)/shard_map/ppermute | solution.py:50
  34.1 1.6 %collective-permute-done.7 = f32[16,8,128]{2,1,0:T(8,128)S(1)} collective-permute-done((f32[16,8,128]{2,1,0:T(8,128)S(1)}, f32[16,8,128]{2,1,0:T(8,128)S(1)}, u32[]{:S(2)}, u32[]{:S(2)}) %collective-permute-start.7) | collective-permute-done | bytes 65568 | tf_op jit(solution)/shard_map/ppermute | solution.py:50
  35.6 1.6 %collective-permute-done.10 = f32[17,8,128]{2,1,0:T(8,128)S(1)} collective-permute-done((f32[17,8,128]{2,1,0:T(8,128)S(1)}, f32[17,8,128]{2,1,0:T(8,128)S(1)}, u32[]{:S(2)}, u32[]{:S(2)}) %collective-permute-start.10) | collective-permute-done | bytes 69664 | tf_op jit(solution)/shard_map/ppermute | solution.py:50
  37.3 1.2 %collective-permute-start.11 = (f32[9,8,128]{2,1,0:T(8,128)S(1)}, f32[9,8,128]{2,1,0:T(8,128)S(1)}, u32[]{:S(2)}, u32[]{:S(2)}) collective-permute-start(f32[9,8,128]{2,1,0:T(8,128)S(1)} %get-tuple-element.57), channel_id=1, source_target_pairs={{0,8},{1,9},{2,10},{3,11},{4,12},{5,13},{6,14},{7,15},{8,16},{9,17... | collective-permute-start | bytes 110600 | tf_op jit(solution)/shard_map/ppermute | solution.py:50
  38.6 2.6 %collective-permute-start.12 = (f32[9,8,128]{2,1,0:T(8,128)S(1)}, f32[9,8,128]{2,1,0:T(8,128)S(1)}, u32[]{:S(2)}, u32[]{:S(2)}) collective-permute-start(f32[9,8,128]{2,1,0:T(8,128)S(1)} %get-tuple-element.58), channel_id=1, source_target_pairs={{0,16},{1,17},{2,18},{3,19},{4,20},{5,21},{6,22},{7,23},{8,24},{9,... | collective-permute-start | bytes 110600 | tf_op jit(solution)/shard_map/ppermute | solution.py:50
  41.1 1.8 %collective-permute-start.13 = (f32[9,8,128]{2,1,0:T(8,128)S(1)}, f32[9,8,128]{2,1,0:T(8,128)S(1)}, u32[]{:S(2)}, u32[]{:S(2)}) collective-permute-start(f32[9,8,128]{2,1,0:T(8,128)S(1)} %get-tuple-element.59), channel_id=1, source_target_pairs={{0,24},{1,25},{2,26},{3,27},{4,28},{5,29},{6,30},{7,31},{8,0},{9,1... | collective-permute-start | bytes 110600 | tf_op jit(solution)/shard_map/ppermute | solution.py:50
  43.6 1.5 %collective-permute-done.13 = f32[9,8,128]{2,1,0:T(8,128)S(1)} collective-permute-done((f32[9,8,128]{2,1,0:T(8,128)S(1)}, f32[9,8,128]{2,1,0:T(8,128)S(1)}, u32[]{:S(2)}, u32[]{:S(2)}) %collective-permute-start.13) | collective-permute-done | bytes 36896 | tf_op jit(solution)/shard_map/ppermute | solution.py:50
  45.9 3.5 %collective-permute-start.15 = (f32[8,8,128]{2,1,0:T(8,128)S(1)}, f32[8,8,128]{2,1,0:T(8,128)S(1)}, u32[]{:S(2)}, u32[]{:S(2)}) collective-permute-start(f32[8,8,128]{2,1,0:T(8,128)S(1)} %get-tuple-element.48), channel_id=1, source_target_pairs={{0,16},{1,17},{2,18},{3,19},{4,20},{5,21},{6,22},{7,23},{8,24},{9,... | collective-permute-start | bytes 98312 | tf_op jit(solution)/shard_map/ppermute | solution.py:50
  51.6 1.7 %collective-permute-done.16 = f32[8,8,128]{2,1,0:T(8,128)S(1)} collective-permute-done((f32[8,8,128]{2,1,0:T(8,128)S(1)}, f32[8,8,128]{2,1,0:T(8,128)S(1)}, u32[]{:S(2)}, u32[]{:S(2)}) %collective-permute-start.16) | collective-permute-done | bytes 32800 | tf_op jit(solution)/shard_map/ppermute | solution.py:50
  53.4 1.2 %collective-permute-start.17 = (f32[16,8,128]{2,1,0:T(8,128)S(1)}, f32[16,8,128]{2,1,0:T(8,128)S(1)}, u32[]{:S(2)}, u32[]{:S(2)}) collective-permute-start(f32[16,8,128]{2,1,0:T(8,128)S(1)} %get-tuple-element.51), channel_id=1, source_target_pairs={{0,4},{1,3},{2,6},{3,1},{4,0},{5,7},{6,2},{7,5},{8,12},{9,11},{10,... | collective-permute-start | bytes 196616 | tf_op jit(solution)/shard_map/ppermute | solution.py:50
  55.5 2.4 %collective-permute-done.17 = f32[16,8,128]{2,1,0:T(8,128)S(1)} collective-permute-done((f32[16,8,128]{2,1,0:T(8,128)S(1)}, f32[16,8,128]{2,1,0:T(8,128)S(1)}, u32[]{:S(2)}, u32[]{:S(2)}) %collective-permute-start.17) | collective-permute-done | bytes 65568 | tf_op jit(solution)/shard_map/ppermute | solution.py:50
  60.2 2.8 %collective-permute-done.18 = f32[32,8,128]{2,1,0:T(8,128)S(1)} collective-permute-done((f32[32,8,128]{2,1,0:T(8,128)S(1)}, f32[32,8,128]{2,1,0:T(8,128)S(1)}, u32[]{:S(2)}, u32[]{:S(2)}) %collective-permute-start.18) | collective-permute-done | bytes 131104 | tf_op jit(solution)/shard_map/ppermute | solution.py:50
  63.0 1.3 %collective-permute-done.21 = f32[32,8,128]{2,1,0:T(8,128)S(1)} collective-permute-done((f32[32,8,128]{2,1,0:T(8,128)S(1)}, f32[32,8,128]{2,1,0:T(8,128)S(1)}, u32[]{:S(2)}, u32[]{:S(2)}) %collective-permute-start.21) | collective-permute-done | bytes 131104 | tf_op jit(solution)/shard_map/ppermute | solution.py:50
  64.6 1.3 %collective-permute-done.22 = f32[64,8,128]{2,1,0:T(8,128)S(1)} collective-permute-done((f32[64,8,128]{2,1,0:T(8,128)S(1)}, f32[64,8,128]{2,1,0:T(8,128)S(1)}, u32[]{:S(2)}, u32[]{:S(2)}) %collective-permute-start.22) | collective-permute-done | bytes 262176 | tf_op jit(solution)/shard_map/ppermute | solution.py:50
  (100 shorter events, 19.2 us)
Async XLA Ops:
  2.4 1.9 %collective-permute-start = (f32[8,64]{1,0:T(8,128)}, f32[8,64]{1,0:T(8,128)S(1)}, u32[]{:S(2)}, u32[]{:S(2)}) collective-permute-start(f32[8,64]{1,0:T(8,128)} %task_stats.1), channel_id=1, source_target_pairs={{0,1},{1,0},{2,3},{3,2},{4,5},{5,4},{6,7},{7,6},{8,9},{9,8},{10,11... | collective-permute-start | bytes 6152 | tf_op jit(solution)/shard_map/ppermute | solution.py:50
  5.1 4.9 %collective-permute-start.1 = (f32[8,64]{1,0:T(8,128)S(1)}, f32[8,64]{1,0:T(8,128)S(1)}, u32[]{:S(2)}, u32[]{:S(2)}) collective-permute-start(f32[8,64]{1,0:T(8,128)S(1)} %add.294), channel_id=1, source_target_pairs={{0,2},{1,3},{2,0},{3,1},{4,6},{5,7},{6,4},{7,5},{8,10},{9,11},{10,... | collective-permute-start | bytes 6152 | tf_op jit(solution)/shard_map/ppermute | solution.py:50
  10.0 4.0 %collective-permute-start.2 = (f32[8,64]{1,0:T(8,128)S(1)}, f32[8,64]{1,0:T(8,128)S(1)}, u32[]{:S(2)}, u32[]{:S(2)}) collective-permute-start(f32[8,64]{1,0:T(8,128)S(1)} %add.297), channel_id=1, source_target_pairs={{0,4},{1,5},{2,6},{3,7},{4,0},{5,1},{6,2},{7,3},{8,12},{9,13},{10,... | collective-permute-start | bytes 6152 | tf_op jit(solution)/shard_map/ppermute | solution.py:50
  14.0 4.0 %collective-permute-start.3 = (f32[8,64]{1,0:T(8,128)S(1)}, f32[8,64]{1,0:T(8,128)S(1)}, u32[]{:S(2)}, u32[]{:S(2)}) collective-permute-start(f32[8,64]{1,0:T(8,128)S(1)} %add.300), channel_id=1, source_target_pairs={{0,8},{1,9},{2,10},{3,11},{4,12},{5,13},{6,14},{7,15},{8,0},{9,1},... | collective-permute-start | bytes 6152 | tf_op jit(solution)/shard_map/ppermute | solution.py:50
  18.1 4.6 %collective-permute-start.4 = (f32[8,64]{1,0:T(8,128)S(1)}, f32[8,64]{1,0:T(8,128)S(1)}, u32[]{:S(2)}, u32[]{:S(2)}) collective-permute-start(f32[8,64]{1,0:T(8,128)S(1)} %add.303), channel_id=1, source_target_pairs={{0,16},{1,17},{2,18},{3,19},{4,20},{5,21},{6,22},{7,23},{8,24},{9,... | collective-permute-start | bytes 6152 | tf_op jit(solution)/shard_map/ppermute | solution.py:50
  22.8 22.4 %copy-start.3 = (f32[1024]{0:T(1024)}, f32[1024]{0:T(1024)S(1)}, u32[]{:S(2)}) copy-start(f32[1024]{0:T(1024)S(1)} %select_reduce_fusion.1) | copy-start | bytes 12292
  24.6 1.6 %collective-permute-start.5 = (f32[64,8,128]{2,1,0:T(8,128)S(1)}, f32[64,8,128]{2,1,0:T(8,128)S(1)}, u32[]{:S(2)}, u32[]{:S(2)}) collective-permute-start(f32[64,8,128]{2,1,0:T(8,128)S(1)} %constant_dynamic-slice_fusion.5), channel_id=1, source_target_pairs={{0,1},{1,0},{2,3},{3,2},{4,5},{5,4},{6,7},{7,6},{8,9},{9,8},{10,11... | collective-permute-start | bytes 786440 | tf_op jit(solution)/shard_map/ppermute | solution.py:50
  24.8 2.6 %collective-permute-start.8 = (f32[65,8,128]{2,1,0:T(8,128)S(1)}, f32[65,8,128]{2,1,0:T(8,128)S(1)}, u32[]{:S(2)}, u32[]{:S(2)}) collective-permute-start(f32[65,8,128]{2,1,0:T(8,128)S(1)} %select_maximum_fusion), channel_id=1, source_target_pairs={{0,1},{1,0},{2,3},{3,2},{4,5},{5,4},{6,7},{7,6},{8,9},{9,8},{10,11... | collective-permute-start | bytes 798728 | tf_op jit(solution)/shard_map/ppermute | solution.py:50
  26.2 5.0 %collective-permute-start.6 = (f32[32,8,128]{2,1,0:T(8,128)S(1)}, f32[32,8,128]{2,1,0:T(8,128)S(1)}, u32[]{:S(2)}, u32[]{:S(2)}) collective-permute-start(f32[32,8,128]{2,1,0:T(8,128)S(1)} %constant_dynamic-slice_fusion.4), channel_id=1, source_target_pairs={{0,2},{1,5},{2,0},{3,7},{4,6},{5,1},{6,4},{7,3},{8,10},{9,13},{10,... | collective-permute-start | bytes 393224 | tf_op jit(solution)/shard_map/ppermute | solution.py:50
  27.7 5.1 %collective-permute-start.9 = (f32[33,8,128]{2,1,0:T(8,128)S(1)}, f32[33,8,128]{2,1,0:T(8,128)S(1)}, u32[]{:S(2)}, u32[]{:S(2)}) collective-permute-start(f32[33,8,128]{2,1,0:T(8,128)S(1)} %pad_maximum_fusion.1), channel_id=1, source_target_pairs={{0,2},{1,5},{2,0},{3,7},{4,6},{5,1},{6,4},{7,3},{8,10},{9,13},{10,... | collective-permute-start | bytes 405512 | tf_op jit(solution)/shard_map/ppermute | solution.py:50
  31.3 4.3 %collective-permute-start.7 = (f32[16,8,128]{2,1,0:T(8,128)S(1)}, f32[16,8,128]{2,1,0:T(8,128)S(1)}, u32[]{:S(2)}, u32[]{:S(2)}) collective-permute-start(f32[16,8,128]{2,1,0:T(8,128)S(1)} %constant_dynamic-slice_fusion.3), channel_id=1, source_target_pairs={{0,4},{1,3},{2,6},{3,1},{4,0},{5,7},{6,2},{7,5},{8,12},{9,11},{10,... | collective-permute-start | bytes 196616 | tf_op jit(solution)/shard_map/ppermute | solution.py:50
  32.8 4.4 %collective-permute-start.10 = (f32[17,8,128]{2,1,0:T(8,128)S(1)}, f32[17,8,128]{2,1,0:T(8,128)S(1)}, u32[]{:S(2)}, u32[]{:S(2)}) collective-permute-start(f32[17,8,128]{2,1,0:T(8,128)S(1)} %pad_maximum_fusion.2), channel_id=1, source_target_pairs={{0,4},{1,3},{2,6},{3,1},{4,0},{5,7},{6,2},{7,5},{8,12},{9,11},{10,... | collective-permute-start | bytes 208904 | tf_op jit(solution)/shard_map/ppermute | solution.py:50
  37.3 5.8 %collective-permute-start.11 = (f32[9,8,128]{2,1,0:T(8,128)S(1)}, f32[9,8,128]{2,1,0:T(8,128)S(1)}, u32[]{:S(2)}, u32[]{:S(2)}) collective-permute-start(f32[9,8,128]{2,1,0:T(8,128)S(1)} %get-tuple-element.57), channel_id=1, source_target_pairs={{0,8},{1,9},{2,10},{3,11},{4,12},{5,13},{6,14},{7,15},{8,16},{9,17... | collective-permute-start | bytes 110600 | tf_op jit(solution)/shard_map/ppermute | solution.py:50
  38.6 5.0 %collective-permute-start.12 = (f32[9,8,128]{2,1,0:T(8,128)S(1)}, f32[9,8,128]{2,1,0:T(8,128)S(1)}, u32[]{:S(2)}, u32[]{:S(2)}) collective-permute-start(f32[9,8,128]{2,1,0:T(8,128)S(1)} %get-tuple-element.58), channel_id=1, source_target_pairs={{0,16},{1,17},{2,18},{3,19},{4,20},{5,21},{6,22},{7,23},{8,24},{9,... | collective-permute-start | bytes 110600 | tf_op jit(solution)/shard_map/ppermute | solution.py:50
  41.1 4.0 %collective-permute-start.13 = (f32[9,8,128]{2,1,0:T(8,128)S(1)}, f32[9,8,128]{2,1,0:T(8,128)S(1)}, u32[]{:S(2)}, u32[]{:S(2)}) collective-permute-start(f32[9,8,128]{2,1,0:T(8,128)S(1)} %get-tuple-element.59), channel_id=1, source_target_pairs={{0,24},{1,25},{2,26},{3,27},{4,28},{5,29},{6,30},{7,31},{8,0},{9,1... | collective-permute-start | bytes 110600 | tf_op jit(solution)/shard_map/ppermute | solution.py:50
  45.2 5.8 %collective-permute-start.14 = (f32[8,8,128]{2,1,0:T(8,128)S(1)}, f32[8,8,128]{2,1,0:T(8,128)S(1)}, u32[]{:S(2)}, u32[]{:S(2)}) collective-permute-start(f32[8,8,128]{2,1,0:T(8,128)S(1)} %get-tuple-element.48), channel_id=1, source_target_pairs={{0,8},{1,9},{2,10},{3,11},{4,12},{5,13},{6,14},{7,15},{8,16},{9,17... | collective-permute-start | bytes 98312 | tf_op jit(solution)/shard_map/ppermute | solution.py:50
  45.9 5.7 %collective-permute-start.15 = (f32[8,8,128]{2,1,0:T(8,128)S(1)}, f32[8,8,128]{2,1,0:T(8,128)S(1)}, u32[]{:S(2)}, u32[]{:S(2)}) collective-permute-start(f32[8,8,128]{2,1,0:T(8,128)S(1)} %get-tuple-element.48), channel_id=1, source_target_pairs={{0,16},{1,17},{2,18},{3,19},{4,20},{5,21},{6,22},{7,23},{8,24},{9,... | collective-permute-start | bytes 98312 | tf_op jit(solution)/shard_map/ppermute | solution.py:50
  49.5 3.9 %collective-permute-start.16 = (f32[8,8,128]{2,1,0:T(8,128)S(1)}, f32[8,8,128]{2,1,0:T(8,128)S(1)}, u32[]{:S(2)}, u32[]{:S(2)}) collective-permute-start(f32[8,8,128]{2,1,0:T(8,128)S(1)} %get-tuple-element.48), channel_id=1, source_target_pairs={{0,24},{1,25},{2,26},{3,27},{4,28},{5,29},{6,30},{7,31},{8,0},{9,1... | collective-permute-start | bytes 98312 | tf_op jit(solution)/shard_map/ppermute | solution.py:50
  53.4 4.5 %collective-permute-start.17 = (f32[16,8,128]{2,1,0:T(8,128)S(1)}, f32[16,8,128]{2,1,0:T(8,128)S(1)}, u32[]{:S(2)}, u32[]{:S(2)}) collective-permute-start(f32[16,8,128]{2,1,0:T(8,128)S(1)} %get-tuple-element.51), channel_id=1, source_target_pairs={{0,4},{1,3},{2,6},{3,1},{4,0},{5,7},{6,2},{7,5},{8,12},{9,11},{10,... | collective-permute-start | bytes 196616 | tf_op jit(solution)/shard_map/ppermute | solution.py:50
  54.6 4.5 %collective-permute-start.20 = (f32[16,8,128]{2,1,0:T(8,128)S(1)}, f32[16,8,128]{2,1,0:T(8,128)S(1)}, u32[]{:S(2)}, u32[]{:S(2)}) collective-permute-start(f32[16,8,128]{2,1,0:T(8,128)S(1)} %get-tuple-element.53), channel_id=1, source_target_pairs={{0,4},{1,3},{2,6},{3,1},{4,0},{5,7},{6,2},{7,5},{8,12},{9,11},{10,... | collective-permute-start | bytes 196616 | tf_op jit(solution)/shard_map/ppermute | solution.py:50
  57.9 5.0 %collective-permute-start.18 = (f32[32,8,128]{2,1,0:T(8,128)S(1)}, f32[32,8,128]{2,1,0:T(8,128)S(1)}, u32[]{:S(2)}, u32[]{:S(2)}) collective-permute-start(f32[32,8,128]{2,1,0:T(8,128)S(1)} %constant_dynamic-update-slice_fusion.10), channel_id=1, source_target_pairs={{0,2},{1,5},{2,0},{3,7},{4,6},{5,1},{6,4},{7,3},{8,10},{9,13},{10,... | collective-permute-start | bytes 393224 | tf_op jit(solution)/shard_map/ppermute | solution.py:50
  59.1 5.2 %collective-permute-start.21 = (f32[32,8,128]{2,1,0:T(8,128)S(1)}, f32[32,8,128]{2,1,0:T(8,128)S(1)}, u32[]{:S(2)}, u32[]{:S(2)}) collective-permute-start(f32[32,8,128]{2,1,0:T(8,128)S(1)} %constant_dynamic-update-slice_fusion.4), channel_id=1, source_target_pairs={{0,2},{1,5},{2,0},{3,7},{4,6},{5,1},{6,4},{7,3},{8,10},{9,13},{10,... | collective-permute-start | bytes 393224 | tf_op jit(solution)/shard_map/ppermute | solution.py:50
  63.0 1.6 %collective-permute-start.19 = (f32[64,8,128]{2,1,0:T(8,128)S(1)}, f32[64,8,128]{2,1,0:T(8,128)S(1)}, u32[]{:S(2)}, u32[]{:S(2)}) collective-permute-start(f32[64,8,128]{2,1,0:T(8,128)S(1)} %constant_dynamic-update-slice_fusion.8), channel_id=1, source_target_pairs={{0,1},{1,0},{2,3},{3,2},{4,5},{5,4},{6,7},{7,6},{8,9},{9,8},{10,11... | collective-permute-start | bytes 786440 | tf_op jit(solution)/shard_map/ppermute | solution.py:50
  64.4 1.6 %collective-permute-start.22 = (f32[64,8,128]{2,1,0:T(8,128)S(1)}, f32[64,8,128]{2,1,0:T(8,128)S(1)}, u32[]{:S(2)}, u32[]{:S(2)}) collective-permute-start(f32[64,8,128]{2,1,0:T(8,128)S(1)} %constant_dynamic-update-slice_fusion.2), channel_id=1, source_target_pairs={{0,1},{1,0},{2,3},{3,2},{4,5},{5,4},{6,7},{7,6},{8,9},{9,8},{10,11... | collective-permute-start | bytes 786440 | tf_op jit(solution)/shard_map/ppermute | solution.py:50
  (5 other events, 87.5 us)

commit v4 on v3

--- a/solution.py
+++ b/solution.py
@@ -2,6 +2,7 @@
 import jax.numpy as jnp
 from jax import lax
 from jax.experimental import pallas as pl
+from jax.experimental.pallas import tpu as pltpu
 from jax.sharding import PartitionSpec as P
 
 LANES = 128
@@ -20,6 +21,12 @@
         rounds.append((stride, radix))
         stride *= radix
     return rounds
+
+
+def row_edges(tokens, rounds):
+    shares = [3,3,3,7]
+    weights = [0] * (rounds - len(shares)) + shares if rounds >= len(shares) else [1] * rounds
+    return [tokens * sum(weights[:at]) // sum(weights) for at in range(rounds + 1)]
 
 
 def wide_rounds(dp, seq):
@@ -121,7 +128,7 @@
 def local_stats(returns, task_bins, loss_mask, tasks):
     return pl.pallas_call(
         stats_kernel,
-        out_shape=jax.ShapeDtypeStruct((SUBLANES, tasks), jnp.float32),
+        out_shape=pltpu.VMEM((SUBLANES, tasks), jnp.float32),
         name="task_stats",
     )(returns.reshape(1, -1), task_bins.reshape(1, -1), loss_mask.reshape(1, -1))
 
@@ -138,13 +145,13 @@
     stats = local_stats(returns, task_bins, loss_mask, tasks)
     chosen = (bins[:, None] == bins_iota).astype(jnp.float32)
     exchanges = small_rounds(dp * seq)
-    parts = len(exchanges) - 1
-    edges = [states.shape[0] * at // parts for at in range(parts + 1)]
+    tokens = states.shape[0]
+    edges = row_edges(tokens, len(exchanges))
     pieces = []
     for at, (stride, radix) in enumerate(exchanges):
         got = [shift(stats, (stride, stride), radix, by) for by in range(1, radix)]
-        if at:
-            rows = slice(edges[at - 1], edges[at])
+        rows = slice(edges[at], edges[at + 1])
+        if rows.start < rows.stop:
             bias, stats = lax.optimization_barrier((value_bias, stats))
             scores = jnp.dot(states[rows], value_weight, preferred_element_type=jnp.float32)
             picked = jnp.sum((scores + bias) * chosen[rows], axis=-1)

time: 67.3 us -> 66.1 us (0.982)
  matrix products: 9.57 us -> 11.1 us
  waiting for transfers between devices: 21.2 us -> 19.8 us
  other arithmetic: 3.88 us -> 3.1 us
    dot_general x4, matrix products: 7.89 us -> 9.38 us  [on_device(): jnp.dot(states[rows], value_weight, preferred_element_type=jnp.float32)]
    ppermute x23, waiting for transfers between devices: 21.2 us -> 19.8 us  [shift(): return lax.ppermute(value, AXES, pairs)]
    add x5, other arithmetic: 0.86 us -> 0.02 us  [on_device(): stats = stats + piece]
  transfers between devices with their start and end apart: 23 -> 23, of which waited for: 16 -> 15; matrix products, arithmetic and copies ran while one was open for 16% -> 18% of each run, Pallas kernels for 0% -> 0%
where the time goes in v4:
time: 66.1 us; the launch traced here: 65.8 us
  starting transfers between devices  28.4 us (43%)
  waiting for transfers between devices  19.8 us (30%)
  matrix products  11.1 us (17%)
  other arithmetic  3.1 us (5%)
  local copies, waits for them, and re-layouts  1.19 us (2%)
  between operations  1.12 us (2%)
  Pallas kernels  1.09 us (2%)
    ppermute x23, starting transfers between devices, shift(): return lax.ppermute(value, AXES, pairs)  28.4 us
    ppermute x23, waiting for transfers between devices, shift(): return lax.ppermute(value, AXES, pairs)  19.8 us
    dot_general x4, matrix products, on_device(): jnp.dot(states[rows], value_weight, preferred_element_type=jnp.float32)  9.38 us
    dot_general x2, matrix products, on_device(): lax.dot_general(states[:, columns], coefficient_low, (((0,), (0,)), ((),...  1.68 us
  transfers between devices with their start and end apart: 23, of which 15 were waited for; matrix products, arithmetic and copies ran while one was open for 18% of the time, Pallas kernels for 0%

profile of v4, /device:TPU:0, one launch (start us, length us, event | category | flops | bytes accessed | tf_op | source)
XLA Modules:
  0.0 65.8 jit_solution(1180725027569415365)
XLA Ops:
  3.7 2.7 %collective-permute-start.1 = (f32[8,64]{1,0:T(8,128)S(1)}, f32[8,64]{1,0:T(8,128)S(1)}, u32[]{:S(2)}, u32[]{:S(2)}) collective-permute-start(f32[8,64]{1,0:T(8,128)S(1)} %add.294), channel_id=1, source_target_pairs={{0,2},{1,3},{2,0},{3,1},{4,6},{5,7},{6,4},{7,5},{8,10},{9,11},{10,... | collective-permute-start | bytes 6152 | tf_op jit(solution)/shard_map/ppermute | solution.py:57
  6.4 2.1 %fusion.56 = f32[192]{0:T(256)S(1)} fusion(f32[1024,64]{0,1:T(8,128)S(1)} %fusion.49, f32[64]{0:T(128)} %param.10, bf16[4096,64]{0,1:T(8,128)(2,1)S(1)} %copy-done, bf16[1,1024,4096]{2,1,0:T(8,128)(2,1)} %param.8), kind=kOutput, calls=%fused_computation.57 | convolution fusion | flops 100699968 | bytes 2147584 | tf_op jit(solution)/shard_map/dot_general | solution.py:156
  8.5 2.2 %collective-permute-start.2 = (f32[8,64]{1,0:T(8,128)S(1)}, f32[8,64]{1,0:T(8,128)S(1)}, u32[]{:S(2)}, u32[]{:S(2)}) collective-permute-start(f32[8,64]{1,0:T(8,128)S(1)} %add.297), channel_id=1, source_target_pairs={{0,4},{1,5},{2,6},{3,7},{4,0},{5,1},{6,2},{7,3},{8,12},{9,13},{10,... | collective-permute-start | bytes 6152 | tf_op jit(solution)/shard_map/ppermute | solution.py:57
  10.7 2.1 %fusion.46 = f32[192]{0:T(256)S(1)} fusion(bf16[4096,64]{0,1:T(8,128)(2,1)S(1)} %copy-done, bf16[1,1024,4096]{2,1,0:T(8,128)(2,1)} %param.8, f32[1024,64]{0,1:T(8,128)S(1)} %fusion.49, f32[64]{0:T(128)} %param.10), kind=kOutput, calls=%fused_computation.26 | convolution fusion | flops 100699968 | bytes 2147584 | tf_op jit(solution)/shard_map/dot_general | solution.py:156
  12.8 1.6 %collective-permute-start.3 = (f32[8,64]{1,0:T(8,128)S(1)}, f32[8,64]{1,0:T(8,128)S(1)}, u32[]{:S(2)}, u32[]{:S(2)}) collective-permute-start(f32[8,64]{1,0:T(8,128)S(1)} %add.300), channel_id=1, source_target_pairs={{0,8},{1,9},{2,10},{3,11},{4,12},{5,13},{6,14},{7,15},{8,0},{9,1},... | collective-permute-start | bytes 6152 | tf_op jit(solution)/shard_map/ppermute | solution.py:57
  14.4 2.0 %fusion.43 = f32[192]{0:T(256)S(1)} fusion(bf16[4096,64]{0,1:T(8,128)(2,1)S(1)} %copy-done, bf16[1,1024,4096]{2,1,0:T(8,128)(2,1)} %param.8, f32[1024,64]{0,1:T(8,128)S(1)} %fusion.49, f32[64]{0:T(128)} %param.10), kind=kOutput, calls=%fused_computation.25 | convolution fusion | flops 100699968 | bytes 2147584 | tf_op jit(solution)/shard_map/dot_general | solution.py:156
  16.5 2.7 %collective-permute-start.4 = (f32[8,64]{1,0:T(8,128)S(1)}, f32[8,64]{1,0:T(8,128)S(1)}, u32[]{:S(2)}, u32[]{:S(2)}) collective-permute-start(f32[8,64]{1,0:T(8,128)S(1)} %add.303), channel_id=1, source_target_pairs={{0,16},{1,17},{2,18},{3,19},{4,20},{5,21},{6,22},{7,23},{8,24},{9,... | collective-permute-start | bytes 6152 | tf_op jit(solution)/shard_map/ppermute | solution.py:57
  19.2 3.2 %fusion.28 = f32[448]{0:T(512)S(1)} fusion(bf16[4096,64]{0,1:T(8,128)(2,1)S(1)} %copy-done, bf16[1,1024,4096]{2,1,0:T(8,128)(2,1)} %param.8, f32[1024,64]{0,1:T(8,128)S(1)} %fusion.49, f32[64]{0:T(128)S(1)} %copy-done.5), kind=kOutput, calls=%fused_computation.20 | convolution fusion | flops 234966592 | bytes 4311040 | tf_op jit(solution)/shard_map/dot_general | solution.py:156
  28.5 2.6 %collective-permute-done.6 = f32[32,8,128]{2,1,0:T(8,128)S(1)} collective-permute-done((f32[32,8,128]{2,1,0:T(8,128)S(1)}, f32[32,8,128]{2,1,0:T(8,128)S(1)}, u32[]{:S(2)}, u32[]{:S(2)}) %collective-permute-start.6) | collective-permute-done | bytes 131104 | tf_op jit(solution)/shard_map/ppermute | solution.py:57
  31.1 1.5 %collective-permute-start.7 = (f32[16,8,128]{2,1,0:T(8,128)S(1)}, f32[16,8,128]{2,1,0:T(8,128)S(1)}, u32[]{:S(2)}, u32[]{:S(2)}) collective-permute-start(f32[16,8,128]{2,1,0:T(8,128)S(1)} %constant_dynamic-slice_fusion.3), channel_id=1, source_target_pairs={{0,4},{1,3},{2,6},{3,1},{4,0},{5,7},{6,2},{7,5},{8,12},{9,11},{10,... | collective-permute-start | bytes 196616 | tf_op jit(solution)/shard_map/ppermute | solution.py:57
  32.8 1.4 %collective-permute-start.10 = (f32[17,8,128]{2,1,0:T(8,128)S(1)}, f32[17,8,128]{2,1,0:T(8,128)S(1)}, u32[]{:S(2)}, u32[]{:S(2)}) collective-permute-start(f32[17,8,128]{2,1,0:T(8,128)S(1)} %pad_maximum_fusion.2), channel_id=1, source_target_pairs={{0,4},{1,3},{2,6},{3,1},{4,0},{5,7},{6,2},{7,5},{8,12},{9,11},{10,... | collective-permute-start | bytes 208904 | tf_op jit(solution)/shard_map/ppermute | solution.py:57
  34.2 1.3 %collective-permute-done.7 = f32[16,8,128]{2,1,0:T(8,128)S(1)} collective-permute-done((f32[16,8,128]{2,1,0:T(8,128)S(1)}, f32[16,8,128]{2,1,0:T(8,128)S(1)}, u32[]{:S(2)}, u32[]{:S(2)}) %collective-permute-start.7) | collective-permute-done | bytes 65568 | tf_op jit(solution)/shard_map/ppermute | solution.py:57
  35.5 1.6 %collective-permute-done.10 = f32[17,8,128]{2,1,0:T(8,128)S(1)} collective-permute-done((f32[17,8,128]{2,1,0:T(8,128)S(1)}, f32[17,8,128]{2,1,0:T(8,128)S(1)}, u32[]{:S(2)}, u32[]{:S(2)}) %collective-permute-start.10) | collective-permute-done | bytes 69664 | tf_op jit(solution)/shard_map/ppermute | solution.py:57
  37.3 1.5 %collective-permute-start.11 = (f32[9,8,128]{2,1,0:T(8,128)S(1)}, f32[9,8,128]{2,1,0:T(8,128)S(1)}, u32[]{:S(2)}, u32[]{:S(2)}) collective-permute-start(f32[9,8,128]{2,1,0:T(8,128)S(1)} %get-tuple-element.57), channel_id=1, source_target_pairs={{0,8},{1,9},{2,10},{3,11},{4,12},{5,13},{6,14},{7,15},{8,16},{9,17... | collective-permute-start | bytes 110600 | tf_op jit(solution)/shard_map/ppermute | solution.py:57
  38.8 1.3 %collective-permute-start.12 = (f32[9,8,128]{2,1,0:T(8,128)S(1)}, f32[9,8,128]{2,1,0:T(8,128)S(1)}, u32[]{:S(2)}, u32[]{:S(2)}) collective-permute-start(f32[9,8,128]{2,1,0:T(8,128)S(1)} %get-tuple-element.58), channel_id=1, source_target_pairs={{0,16},{1,17},{2,18},{3,19},{4,20},{5,21},{6,22},{7,23},{8,24},{9,... | collective-permute-start | bytes 110600 | tf_op jit(solution)/shard_map/ppermute | solution.py:57
  40.1 1.4 %collective-permute-start.13 = (f32[9,8,128]{2,1,0:T(8,128)S(1)}, f32[9,8,128]{2,1,0:T(8,128)S(1)}, u32[]{:S(2)}, u32[]{:S(2)}) collective-permute-start(f32[9,8,128]{2,1,0:T(8,128)S(1)} %get-tuple-element.59), channel_id=1, source_target_pairs={{0,24},{1,25},{2,26},{3,27},{4,28},{5,29},{6,30},{7,31},{8,0},{9,1... | collective-permute-start | bytes 110600 | tf_op jit(solution)/shard_map/ppermute | solution.py:57
  41.5 1.6 %collective-permute-done.11 = f32[9,8,128]{2,1,0:T(8,128)S(1)} collective-permute-done((f32[9,8,128]{2,1,0:T(8,128)S(1)}, f32[9,8,128]{2,1,0:T(8,128)S(1)}, u32[]{:S(2)}, u32[]{:S(2)}) %collective-permute-start.11) | collective-permute-done | bytes 36896 | tf_op jit(solution)/shard_map/ppermute | solution.py:57
  44.3 1.5 %collective-permute-start.14 = (f32[8,8,128]{2,1,0:T(8,128)S(1)}, f32[8,8,128]{2,1,0:T(8,128)S(1)}, u32[]{:S(2)}, u32[]{:S(2)}) collective-permute-start(f32[8,8,128]{2,1,0:T(8,128)S(1)} %get-tuple-element.48), channel_id=1, source_target_pairs={{0,8},{1,9},{2,10},{3,11},{4,12},{5,13},{6,14},{7,15},{8,16},{9,17... | collective-permute-start | bytes 98312 | tf_op jit(solution)/shard_map/ppermute | solution.py:57
  45.8 2.2 %collective-permute-start.15 = (f32[8,8,128]{2,1,0:T(8,128)S(1)}, f32[8,8,128]{2,1,0:T(8,128)S(1)}, u32[]{:S(2)}, u32[]{:S(2)}) collective-permute-start(f32[8,8,128]{2,1,0:T(8,128)S(1)} %get-tuple-element.48), channel_id=1, source_target_pairs={{0,16},{1,17},{2,18},{3,19},{4,20},{5,21},{6,22},{7,23},{8,24},{9,... | collective-permute-start | bytes 98312 | tf_op jit(solution)/shard_map/ppermute | solution.py:57
  52.0 1.4 %collective-permute-start.17 = (f32[16,8,128]{2,1,0:T(8,128)S(1)}, f32[16,8,128]{2,1,0:T(8,128)S(1)}, u32[]{:S(2)}, u32[]{:S(2)}) collective-permute-start(f32[16,8,128]{2,1,0:T(8,128)S(1)} %get-tuple-element.51), channel_id=1, source_target_pairs={{0,4},{1,3},{2,6},{3,1},{4,0},{5,7},{6,2},{7,5},{8,12},{9,11},{10,... | collective-permute-start | bytes 196616 | tf_op jit(solution)/shard_map/ppermute | solution.py:57
  54.1 2.5 %collective-permute-done.17 = f32[16,8,128]{2,1,0:T(8,128)S(1)} collective-permute-done((f32[16,8,128]{2,1,0:T(8,128)S(1)}, f32[16,8,128]{2,1,0:T(8,128)S(1)}, u32[]{:S(2)}, u32[]{:S(2)}) %collective-permute-start.17) | collective-permute-done | bytes 65568 | tf_op jit(solution)/shard_map/ppermute | solution.py:57
  58.9 2.8 %collective-permute-done.18 = f32[32,8,128]{2,1,0:T(8,128)S(1)} collective-permute-done((f32[32,8,128]{2,1,0:T(8,128)S(1)}, f32[32,8,128]{2,1,0:T(8,128)S(1)}, u32[]{:S(2)}, u32[]{:S(2)}) %collective-permute-start.18) | collective-permute-done | bytes 131104 | tf_op jit(solution)/shard_map/ppermute | solution.py:57
  61.8 1.3 %collective-permute-done.21 = f32[32,8,128]{2,1,0:T(8,128)S(1)} collective-permute-done((f32[32,8,128]{2,1,0:T(8,128)S(1)}, f32[32,8,128]{2,1,0:T(8,128)S(1)}, u32[]{:S(2)}, u32[]{:S(2)}) %collective-permute-start.21) | collective-permute-done | bytes 131104 | tf_op jit(solution)/shard_map/ppermute | solution.py:57
  63.4 1.3 %collective-permute-done.22 = f32[64,8,128]{2,1,0:T(8,128)S(1)} collective-permute-done((f32[64,8,128]{2,1,0:T(8,128)S(1)}, f32[64,8,128]{2,1,0:T(8,128)S(1)}, u32[]{:S(2)}, u32[]{:S(2)}) %collective-permute-start.22) | collective-permute-done | bytes 262176 | tf_op jit(solution)/shard_map/ppermute | solution.py:57
  (100 shorter events, 18.7 us)
Async XLA Ops:
  0.6 21.8 %copy-start.1 = (s32[1,1024]{1,0:T(1,128)S(1)}, s32[1,1024]{1,0:T(1,128)}, u32[]{:S(2)}) copy-start(s32[1,1024]{1,0:T(1,128)} %bins_ref.1) | copy-start | bytes 12292
  1.8 1.9 %collective-permute-start = (f32[8,64]{1,0:T(8,128)S(1)}, f32[8,64]{1,0:T(8,128)S(1)}, u32[]{:S(2)}, u32[]{:S(2)}) collective-permute-start(f32[8,64]{1,0:T(8,128)S(1)} %task_stats.1), channel_id=1, source_target_pairs={{0,1},{1,0},{2,3},{3,2},{4,5},{5,4},{6,7},{7,6},{8,9},{9,8},{10,11... | collective-permute-start | bytes 6152 | tf_op jit(solution)/shard_map/ppermute | solution.py:57
  3.7 4.8 %collective-permute-start.1 = (f32[8,64]{1,0:T(8,128)S(1)}, f32[8,64]{1,0:T(8,128)S(1)}, u32[]{:S(2)}, u32[]{:S(2)}) collective-permute-start(f32[8,64]{1,0:T(8,128)S(1)} %add.294), channel_id=1, source_target_pairs={{0,2},{1,3},{2,0},{3,1},{4,6},{5,7},{6,4},{7,5},{8,10},{9,11},{10,... | collective-permute-start | bytes 6152 | tf_op jit(solution)/shard_map/ppermute | solution.py:57
  8.5 4.3 %collective-permute-start.2 = (f32[8,64]{1,0:T(8,128)S(1)}, f32[8,64]{1,0:T(8,128)S(1)}, u32[]{:S(2)}, u32[]{:S(2)}) collective-permute-start(f32[8,64]{1,0:T(8,128)S(1)} %add.297), channel_id=1, source_target_pairs={{0,4},{1,5},{2,6},{3,7},{4,0},{5,1},{6,2},{7,3},{8,12},{9,13},{10,... | collective-permute-start | bytes 6152 | tf_op jit(solution)/shard_map/ppermute | solution.py:57
  12.8 3.7 %collective-permute-start.3 = (f32[8,64]{1,0:T(8,128)S(1)}, f32[8,64]{1,0:T(8,128)S(1)}, u32[]{:S(2)}, u32[]{:S(2)}) collective-permute-start(f32[8,64]{1,0:T(8,128)S(1)} %add.300), channel_id=1, source_target_pairs={{0,8},{1,9},{2,10},{3,11},{4,12},{5,13},{6,14},{7,15},{8,0},{9,1},... | collective-permute-start | bytes 6152 | tf_op jit(solution)/shard_map/ppermute | solution.py:57
  16.5 5.9 %collective-permute-start.4 = (f32[8,64]{1,0:T(8,128)S(1)}, f32[8,64]{1,0:T(8,128)S(1)}, u32[]{:S(2)}, u32[]{:S(2)}) collective-permute-start(f32[8,64]{1,0:T(8,128)S(1)} %add.303), channel_id=1, source_target_pairs={{0,16},{1,17},{2,18},{3,19},{4,20},{5,21},{6,22},{7,23},{8,24},{9,... | collective-permute-start | bytes 6152 | tf_op jit(solution)/shard_map/ppermute | solution.py:57
  24.4 1.6 %collective-permute-start.5 = (f32[64,8,128]{2,1,0:T(8,128)S(1)}, f32[64,8,128]{2,1,0:T(8,128)S(1)}, u32[]{:S(2)}, u32[]{:S(2)}) collective-permute-start(f32[64,8,128]{2,1,0:T(8,128)S(1)} %constant_dynamic-slice_fusion.5), channel_id=1, source_target_pairs={{0,1},{1,0},{2,3},{3,2},{4,5},{5,4},{6,7},{7,6},{8,9},{9,8},{10,11... | collective-permute-start | bytes 786440 | tf_op jit(solution)/shard_map/ppermute | solution.py:57
  24.7 2.3 %collective-permute-start.8 = (f32[65,8,128]{2,1,0:T(8,128)S(1)}, f32[65,8,128]{2,1,0:T(8,128)S(1)}, u32[]{:S(2)}, u32[]{:S(2)}) collective-permute-start(f32[65,8,128]{2,1,0:T(8,128)S(1)} %select_maximum_fusion), channel_id=1, source_target_pairs={{0,1},{1,0},{2,3},{3,2},{4,5},{5,4},{6,7},{7,6},{8,9},{9,8},{10,11... | collective-permute-start | bytes 798728 | tf_op jit(solution)/shard_map/ppermute | solution.py:57
  26.1 5.0 %collective-permute-start.6 = (f32[32,8,128]{2,1,0:T(8,128)S(1)}, f32[32,8,128]{2,1,0:T(8,128)S(1)}, u32[]{:S(2)}, u32[]{:S(2)}) collective-permute-start(f32[32,8,128]{2,1,0:T(8,128)S(1)} %constant_dynamic-slice_fusion.4), channel_id=1, source_target_pairs={{0,2},{1,5},{2,0},{3,7},{4,6},{5,1},{6,4},{7,3},{8,10},{9,13},{10,... | collective-permute-start | bytes 393224 | tf_op jit(solution)/shard_map/ppermute | solution.py:57
  27.3 5.4 %collective-permute-start.9 = (f32[33,8,128]{2,1,0:T(8,128)S(1)}, f32[33,8,128]{2,1,0:T(8,128)S(1)}, u32[]{:S(2)}, u32[]{:S(2)}) collective-permute-start(f32[33,8,128]{2,1,0:T(8,128)S(1)} %pad_maximum_fusion.1), channel_id=1, source_target_pairs={{0,2},{1,5},{2,0},{3,7},{4,6},{5,1},{6,4},{7,3},{8,10},{9,13},{10,... | collective-permute-start | bytes 405512 | tf_op jit(solution)/shard_map/ppermute | solution.py:57
  31.1 4.3 %collective-permute-start.7 = (f32[16,8,128]{2,1,0:T(8,128)S(1)}, f32[16,8,128]{2,1,0:T(8,128)S(1)}, u32[]{:S(2)}, u32[]{:S(2)}) collective-permute-start(f32[16,8,128]{2,1,0:T(8,128)S(1)} %constant_dynamic-slice_fusion.3), channel_id=1, source_target_pairs={{0,4},{1,3},{2,6},{3,1},{4,0},{5,7},{6,2},{7,5},{8,12},{9,11},{10,... | collective-permute-start | bytes 196616 | tf_op jit(solution)/shard_map/ppermute | solution.py:57
  32.8 4.4 %collective-permute-start.10 = (f32[17,8,128]{2,1,0:T(8,128)S(1)}, f32[17,8,128]{2,1,0:T(8,128)S(1)}, u32[]{:S(2)}, u32[]{:S(2)}) collective-permute-start(f32[17,8,128]{2,1,0:T(8,128)S(1)} %pad_maximum_fusion.2), channel_id=1, source_target_pairs={{0,4},{1,3},{2,6},{3,1},{4,0},{5,7},{6,2},{7,5},{8,12},{9,11},{10,... | collective-permute-start | bytes 208904 | tf_op jit(solution)/shard_map/ppermute | solution.py:57
  37.3 5.8 %collective-permute-start.11 = (f32[9,8,128]{2,1,0:T(8,128)S(1)}, f32[9,8,128]{2,1,0:T(8,128)S(1)}, u32[]{:S(2)}, u32[]{:S(2)}) collective-permute-start(f32[9,8,128]{2,1,0:T(8,128)S(1)} %get-tuple-element.57), channel_id=1, source_target_pairs={{0,8},{1,9},{2,10},{3,11},{4,12},{5,13},{6,14},{7,15},{8,16},{9,17... | collective-permute-start | bytes 110600 | tf_op jit(solution)/shard_map/ppermute | solution.py:57
  38.8 5.1 %collective-permute-start.12 = (f32[9,8,128]{2,1,0:T(8,128)S(1)}, f32[9,8,128]{2,1,0:T(8,128)S(1)}, u32[]{:S(2)}, u32[]{:S(2)}) collective-permute-start(f32[9,8,128]{2,1,0:T(8,128)S(1)} %get-tuple-element.58), channel_id=1, source_target_pairs={{0,16},{1,17},{2,18},{3,19},{4,20},{5,21},{6,22},{7,23},{8,24},{9,... | collective-permute-start | bytes 110600 | tf_op jit(solution)/shard_map/ppermute | solution.py:57
  40.1 4.2 %collective-permute-start.13 = (f32[9,8,128]{2,1,0:T(8,128)S(1)}, f32[9,8,128]{2,1,0:T(8,128)S(1)}, u32[]{:S(2)}, u32[]{:S(2)}) collective-permute-start(f32[9,8,128]{2,1,0:T(8,128)S(1)} %get-tuple-element.59), channel_id=1, source_target_pairs={{0,24},{1,25},{2,26},{3,27},{4,28},{5,29},{6,30},{7,31},{8,0},{9,1... | collective-permute-start | bytes 110600 | tf_op jit(solution)/shard_map/ppermute | solution.py:57
  44.3 5.8 %collective-permute-start.14 = (f32[8,8,128]{2,1,0:T(8,128)S(1)}, f32[8,8,128]{2,1,0:T(8,128)S(1)}, u32[]{:S(2)}, u32[]{:S(2)}) collective-permute-start(f32[8,8,128]{2,1,0:T(8,128)S(1)} %get-tuple-element.48), channel_id=1, source_target_pairs={{0,8},{1,9},{2,10},{3,11},{4,12},{5,13},{6,14},{7,15},{8,16},{9,17... | collective-permute-start | bytes 98312 | tf_op jit(solution)/shard_map/ppermute | solution.py:57
  45.8 5.2 %collective-permute-start.15 = (f32[8,8,128]{2,1,0:T(8,128)S(1)}, f32[8,8,128]{2,1,0:T(8,128)S(1)}, u32[]{:S(2)}, u32[]{:S(2)}) collective-permute-start(f32[8,8,128]{2,1,0:T(8,128)S(1)} %get-tuple-element.48), channel_id=1, source_target_pairs={{0,16},{1,17},{2,18},{3,19},{4,20},{5,21},{6,22},{7,23},{8,24},{9,... | collective-permute-start | bytes 98312 | tf_op jit(solution)/shard_map/ppermute | solution.py:57
  48.0 3.9 %collective-permute-start.16 = (f32[8,8,128]{2,1,0:T(8,128)S(1)}, f32[8,8,128]{2,1,0:T(8,128)S(1)}, u32[]{:S(2)}, u32[]{:S(2)}) collective-permute-start(f32[8,8,128]{2,1,0:T(8,128)S(1)} %get-tuple-element.48), channel_id=1, source_target_pairs={{0,24},{1,25},{2,26},{3,27},{4,28},{5,29},{6,30},{7,31},{8,0},{9,1... | collective-permute-start | bytes 98312 | tf_op jit(solution)/shard_map/ppermute | solution.py:57
  52.0 4.6 %collective-permute-start.17 = (f32[16,8,128]{2,1,0:T(8,128)S(1)}, f32[16,8,128]{2,1,0:T(8,128)S(1)}, u32[]{:S(2)}, u32[]{:S(2)}) collective-permute-start(f32[16,8,128]{2,1,0:T(8,128)S(1)} %get-tuple-element.51), channel_id=1, source_target_pairs={{0,4},{1,3},{2,6},{3,1},{4,0},{5,7},{6,2},{7,5},{8,12},{9,11},{10,... | collective-permute-start | bytes 196616 | tf_op jit(solution)/shard_map/ppermute | solution.py:57
  53.4 4.3 %collective-permute-start.20 = (f32[16,8,128]{2,1,0:T(8,128)S(1)}, f32[16,8,128]{2,1,0:T(8,128)S(1)}, u32[]{:S(2)}, u32[]{:S(2)}) collective-permute-start(f32[16,8,128]{2,1,0:T(8,128)S(1)} %get-tuple-element.53), channel_id=1, source_target_pairs={{0,4},{1,3},{2,6},{3,1},{4,0},{5,7},{6,2},{7,5},{8,12},{9,11},{10,... | collective-permute-start | bytes 196616 | tf_op jit(solution)/shard_map/ppermute | solution.py:57
  56.6 5.0 %collective-permute-start.18 = (f32[32,8,128]{2,1,0:T(8,128)S(1)}, f32[32,8,128]{2,1,0:T(8,128)S(1)}, u32[]{:S(2)}, u32[]{:S(2)}) collective-permute-start(f32[32,8,128]{2,1,0:T(8,128)S(1)} %constant_dynamic-update-slice_fusion.10), channel_id=1, source_target_pairs={{0,2},{1,5},{2,0},{3,7},{4,6},{5,1},{6,4},{7,3},{8,10},{9,13},{10,... | collective-permute-start | bytes 393224 | tf_op jit(solution)/shard_map/ppermute | solution.py:57
  57.7 5.4 %collective-permute-start.21 = (f32[32,8,128]{2,1,0:T(8,128)S(1)}, f32[32,8,128]{2,1,0:T(8,128)S(1)}, u32[]{:S(2)}, u32[]{:S(2)}) collective-permute-start(f32[32,8,128]{2,1,0:T(8,128)S(1)} %constant_dynamic-update-slice_fusion.4), channel_id=1, source_target_pairs={{0,2},{1,5},{2,0},{3,7},{4,6},{5,1},{6,4},{7,3},{8,10},{9,13},{10,... | collective-permute-start | bytes 393224 | tf_op jit(solution)/shard_map/ppermute | solution.py:57
  61.7 1.6 %collective-permute-start.19 = (f32[64,8,128]{2,1,0:T(8,128)S(1)}, f32[64,8,128]{2,1,0:T(8,128)S(1)}, u32[]{:S(2)}, u32[]{:S(2)}) collective-permute-start(f32[64,8,128]{2,1,0:T(8,128)S(1)} %constant_dynamic-update-slice_fusion.8), channel_id=1, source_target_pairs={{0,1},{1,0},{2,3},{3,2},{4,5},{5,4},{6,7},{7,6},{8,9},{9,8},{10,11... | collective-permute-start | bytes 786440 | tf_op jit(solution)/shard_map/ppermute | solution.py:57
  63.1 1.6 %collective-permute-start.22 = (f32[64,8,128]{2,1,0:T(8,128)S(1)}, f32[64,8,128]{2,1,0:T(8,128)S(1)}, u32[]{:S(2)}, u32[]{:S(2)}) collective-permute-start(f32[64,8,128]{2,1,0:T(8,128)S(1)} %constant_dynamic-update-slice_fusion.2), channel_id=1, source_target_pairs={{0,1},{1,0},{2,3},{3,2},{4,5},{5,4},{6,7},{7,6},{8,9},{9,8},{10,11... | collective-permute-start | bytes 786440 | tf_op jit(solution)/shard_map/ppermute | solution.py:57
  (5 other events, 86.8 us)
